TPU v7x, 32 devices: a whole 2x2x4 slice. The times are simulated.
32 devices in a mesh: row: 2 (over core), col: 16 (over z, y, x).
Axes of the slice: x: 2, y: 2, z: 4, core: 2. Of those that a mesh axis runs over, the one named last changes fastest.
Arguments:
- observed: bfloat16 [1024, 16, 2048], P(None, 'row', 'col'), may hold values from -40 to 40
- library: bfloat16 [1024, 256], P('col'), may hold values from -0.1875 to 0.1875
Outputs:
- abundance: float32 [256, 16, 2048], P(None, 'row', 'col')
All inputs are finite; a program needn't handle non-finite values.
Results may differ from a plain program's by a relative error of at most 0.0024.
Values may be sent and summed in bfloat16 or wider, within the bound.
No kernel may reach another device: no remote copies, remote signals or barrier semaphores. Data moves between devices by JAX's collectives and lax.ppermute only.
A program may use at most 128 MiB of HBM per device.

v0:
```python
import functools

import jax
import jax.numpy as jnp
from jax import lax
from jax.experimental import pallas as pl
from jax.experimental.pallas import tpu as pltpu
from jax.sharding import PartitionSpec as P

ITERS = 3

prox_tau = 8.0
weight_sparse = 0.3
weight_tv = 1.0

F32 = jnp.float32
BF16 = jnp.bfloat16
SHIFT = 1.0 + prox_tau
GROUP = 8
UNROLL = 16


def split(value):
    high = value.astype(BF16)
    return high, (value - high.astype(F32)).astype(BF16)


def dot(left, right):
    return jnp.dot(left, right, preferred_element_type=F32)


def dot_full(left, right):
    return jnp.dot(left, right, precision=lax.Precision.HIGHEST, preferred_element_type=F32)


def dot_columns(left, right):
    return lax.dot_general(left, right, (((0,), (0,)), ((), ())), preferred_element_type=F32)


def clip(value, bound):
    return jnp.minimum(jnp.maximum(value, -bound), bound)


def call(body, outs, args, scratch=(), flops=0, limit=24):
    return pl.pallas_call(
        body,
        out_shape=[jax.ShapeDtypeStruct(*out) for out in outs],
        in_specs=[pl.BlockSpec(memory_space=pltpu.VMEM)] * len(args),
        out_specs=[pl.BlockSpec(memory_space=pltpu.VMEM)] * len(outs),
        scratch_shapes=list(scratch),
        cost_estimate=pl.CostEstimate(flops=flops, bytes_accessed=0, transcendentals=0),
        compiler_params=pltpu.CompilerParams(vmem_limit_bytes=limit << 20),
    )(*args)


def groups(members, step):
    def body(index, carry):
        return step(pl.multiple_of(index * GROUP, GROUP), carry)

    return body, members // GROUP


def roll(value, shift):
    return pltpu.roll(value, shift % value.shape[1], 1)


def lanes_of(shape):
    return lax.broadcasted_iota(jnp.int32, shape, 1)


def flag(condition):
    return jnp.where(condition, 1.0, 0.0).astype(F32)


def edge_flags():
    row, col = lax.axis_index("row"), lax.axis_index("col")
    return (
        flag(row > 0),
        flag(row < lax.axis_size("row") - 1),
        flag(col > 0),
        flag(col < lax.axis_size("col") - 1),
    )


def invert(gram, inverse, power, left):
    eye = flag(
        lax.broadcasted_iota(jnp.int32, gram.shape, 0) == lax.broadcasted_iota(jnp.int32, gram.shape, 1)
    )
    system = gram + SHIFT * eye
    bound = jnp.max(jnp.sum(jnp.abs(gram), axis=1, keepdims=True)) + SHIFT
    nearest = jnp.sum(system * eye) / jnp.sum(system * system)
    scale = jnp.where(nearest * bound < 1.9, nearest, 2.0 / (bound + SHIFT))
    first = eye - scale * system
    squared = dot_full(first, first)
    inverse[...] = scale * (eye + first)
    power[...] = squared
    left[0] = jnp.sum(squared * squared)

    def step(index, carry):
        @pl.when(left[0] > 0.0)
        def _():
            current = power[...]
            inverse[...] = inverse[...] + dot_full(inverse[...], current)

        @pl.when(left[0] > 1e-6)
        def _():
            current = power[...]
            squared = dot_full(current, current)
            power[...] = squared
            left[1] = jnp.sum(squared * squared)

        left[0] = jnp.where(left[0] > 1e-6, left[1], 0.0)
        return carry

    lax.fori_loop(0, 20, step, 0)


def apply_inverse(inv_high, inv_low, rhs_high, rhs_low, store):
    width = rhs_high.shape[1]
    for start in range(0, width, 512):
        block = min(512, width - start)
        high, low = rhs_high[:, start : start + block], rhs_low[:, start : start + block]
        store(start, block, dot(inv_high[...], high) + (dot(inv_high[...], low) + dot(inv_low[...], high)))


def survey_kernel(rows, cols, observed, columns, row_edge, norm):
    channels, pixels = observed.shape
    spot = lax.broadcasted_iota(jnp.int32, (2 * rows, pixels), 0)
    pixel = lax.broadcasted_iota(jnp.int32, (2 * rows, pixels), 1)
    wanted = jnp.where(spot < rows, spot * cols, (spot - rows) * cols + cols - 1)
    chosen = flag(pixel == wanted).astype(BF16)
    columns[...] = lax.dot_general(
        chosen, observed[...], (((1,), (1,)), ((), ())), preferred_element_type=F32
    ).astype(BF16)
    is_upper = edge_flags()[1] > 0.0

    @pl.when(is_upper)
    def _():
        row_edge[...] = observed[:, pixels - cols :]

    @pl.when(jnp.logical_not(is_upper))
    def _():
        row_edge[...] = observed[:, :cols]

    tall = 2 * GROUP

    def step(index, total):
        here = pl.ds(pl.multiple_of(index * tall, tall), tall)
        total = list(total)
        for i in range(rows):
            value = observed[here, i * cols : (i + 1) * cols].astype(F32)
            total[i % 2] = total[i % 2] + value * value
        return tuple(total)

    zero = jnp.zeros((tall, cols), F32)
    even, odd = lax.fori_loop(0, channels // tall, step, (zero, zero), unroll=8)
    total = even + odd
    norm[...] = total[:GROUP, :] + total[GROUP:, :]


def start_kernel(rows, cols, order, *refs):
    ordered = order is True
    observed, row_halo, left_halo, right_halo = refs[:4]
    inputs = 5 if ordered else 9
    pieces = refs[4:inputs]
    projected, inv_high, inv_low, fit, fit_gram, quad, near_row, near_left, near_right = refs[inputs : inputs + 9]
    inverse, power, rhs_high, rhs_low, left, panel = refs[inputs + 9 : inputs + 15]
    if ordered:
        full = pieces[0]
    else:
        full = refs[inputs + 15]
        place_library(pieces, full, order)
    members = full.shape[1]
    pixels = rows * cols
    panel[...] = jnp.zeros(panel.shape, BF16)
    panel[0 : 2 * rows, :] = right_halo[...]
    panel[2 * rows : 4 * rows, :] = left_halo[...]
    block = min(512, pixels)
    for start in range(0, pixels, block):
        span = slice(start, start + block)
        result = dot_columns(full[...], observed[:, span])
        projected[:, span] = result
        rhs_high[:, span], rhs_low[:, span] = split(result)
    span = slice(pixels, pixels + cols)
    rhs_high[:, span], rhs_low[:, span] = split(dot_columns(full[...], row_halo[...]))
    span = slice(pixels + cols, pixels + cols + panel.shape[0])
    beside = lax.dot_general(full[...], panel[...], (((0,), (1,)), ((), ())), preferred_element_type=F32)
    rhs_high[:, span], rhs_low[:, span] = split(beside)
    invert(dot_columns(full[...], full[...]), inverse, power, left)
    inv_high[...], inv_low[...] = split(inverse[...])

    def store(start, size, value):
        if start < pixels:
            fit[:, start : start + size] = value
        else:
            near_row[...] = value[:, :cols]
            near_right[...] = value[:, cols:]
            near_left[...] = roll(value[:, cols:], -3 * rows)

    apply_inverse(inv_high, inv_low, rhs_high, rhs_low, store)

    def step(base, sums):
        here = pl.ds(base, GROUP)
        total, cross = sums
        for i in range(rows):
            span = slice(i * cols, (i + 1) * cols)
            a, p = fit[here, span], projected[here, span]
            ga = p - SHIFT * a
            fit_gram[here, span] = ga
            total = total + a * (ga - 2.0 * p)
            cross = cross + a * p
        return total, cross

    zero = jnp.zeros((GROUP, cols), F32)
    body, count = groups(members, step)
    total, cross = lax.fori_loop(0, count, body, (zero, zero), unroll=UNROLL)
    quad[0:GROUP, :] = total
    quad[GROUP : 2 * GROUP, :] = cross


def write_edges(base, members, a, b, below, row_edge, left_edge, right_edge):
    here = pl.ds(base, GROUP)
    is_upper = below > 0.0
    row_edge[here, :] = jnp.where(is_upper, a[-1], a[0])
    row_edge[pl.ds(base + members, GROUP), :] = jnp.where(is_upper, b[-1], b[0])
    lane = lanes_of(a[0].shape)
    cols = a[0].shape[1]
    left = jnp.zeros_like(a[0])
    right = jnp.zeros_like(a[0])
    for i, value in enumerate(a + b):
        left = jnp.where(lane == i, roll(value, i), left)
        right = jnp.where(lane == i, roll(value, i + 1 - cols), right)
    left_edge[here, :] = left
    right_edge[here, :] = right


def place_library(pieces, full, order):
    mine, mine_rest, other, other_rest, rows_of = pieces
    rows = rows_of.shape[0]
    own = lax.axis_index("col")
    parity = lax.axis_index("row")
    bits = own
    for _ in range(max(1, (lax.axis_size("col") - 1).bit_length())):
        parity = parity ^ (bits & 1)
        bits = bits >> 1
    half = parity
    blocks = mine.shape[0] // rows
    for offset, first, second in ((0, mine, other), (blocks, mine_rest, other_rest)):
        for block in range(blocks):
            base = (own ^ order[block + offset]) * (2 * rows)
            source = slice(block * rows, (block + 1) * rows)
            full[pl.ds(pl.multiple_of(base + half * rows, rows), rows), :] = first[source, :]
            full[pl.ds(pl.multiple_of(base + (1 - half) * rows, rows), rows), :] = second[source, :]


def new_penalty(scalars, sums):
    penalty = scalars[0:1, 0:1]
    primal = jnp.sum(jnp.sum(sums[0:GROUP, :], axis=0, keepdims=True), axis=1, keepdims=True)
    dual = jnp.sum(jnp.sum(sums[GROUP : 2 * GROUP, :], axis=0, keepdims=True), axis=1, keepdims=True)
    following = penalty * jnp.sqrt(jnp.sqrt((primal + 1.0) / (penalty * penalty * dual + 1.0)))
    return penalty, following, penalty / following


def wide(value, shape):
    return jnp.broadcast_to(value, shape)


def shrink_kernel(rows, cols, first, last, *refs):
    if first:
        fit, quad, norm, row_halo, left_halo, right_halo = refs[:6]
        outs = refs[6:]
    else:
        (fit, other, quad, norm, row_halo, left_halo, right_halo, scalars, sums) = refs[:9]
        (old_sparse, old_down, old_right, old_top, old_side) = refs[9:14]
        outs = refs[14:]
    (estimate, sparse, down_sum, right_sum, top_sum, side_sum, down_arg, right_arg, top_arg, side_arg) = outs[:10]
    residuals, new_scalars = outs[10:12]
    members = fit.shape[0]
    shape = (GROUP, cols)
    if first:
        penalty = jnp.ones((1, 1), F32)
        rescale = jnp.ones((1, 1), F32)
    else:
        before, penalty, rescale = new_penalty(scalars, sums)
        old_bound = wide(weight_tv / before, shape)
        old_sparse_bound = wide(weight_sparse / before, shape)
    new_scalars[0:1, :] = wide(penalty, (1, cols))
    new_scalars[1:2, :] = wide(rescale, (1, cols))
    bound = wide(weight_tv / penalty, shape)
    sparse_bound = wide(weight_sparse / penalty, shape)
    scale = wide(rescale, shape)
    has_above, has_below, has_left, has_right = edge_flags()
    lane = lanes_of(shape)
    keep_last = jnp.where(lane == cols - 1, has_right, 1.0)
    is_panel = jnp.where(lane < rows, has_left, 0.0)

    def mixed(a, b):
        return a + scale * b

    def shrunk(value, old, sums_now):
        primal, dual = sums_now
        if first:
            total = value
        else:
            old_total = old
            old_clip = clip(old_total, old_bound)
            total = value + scale * old_clip
        rest = total - clip(total, bound)
        arg = value - rest
        primal = primal + arg * arg
        change = rest if first else rest - (old_total - old_clip)
        dual = dual + change * change
        return total, arg, (primal, dual)

    def step(base, sums_now):
        here = pl.ds(base, GROUP)
        spans = [slice(i * cols, (i + 1) * cols) for i in range(rows)]
        if first:
            now = [fit[here, span] for span in spans]
            near_row = row_halo[here, :]
            near_left, near_right = left_halo[here, :], right_halo[here, :]
        else:
            now = [mixed(fit[here, span], other[here, span]) for span in spans]
            near_row = mixed(row_halo[here, :], row_halo[pl.ds(base + members, GROUP), :])
            near_left = mixed(left_halo[here, :], roll(left_halo[here, :], -rows))
            near_right = mixed(right_halo[here, :], roll(right_halo[here, :], -rows))
        column = jnp.zeros(shape, F32)
        for i in range(rows):
            value = now[i]
            estimate[here, spans[i]] = value
            column = jnp.where(lane == i, roll(value, i), column)
            primal, dual = sums_now
            if first:
                total = value
            else:
                old = old_sparse[here, spans[i]]
                total = value + scale * jnp.minimum(old, old_sparse_bound)
            kept = jnp.maximum(total - sparse_bound, 0.0)
            sparse[here, spans[i]] = total
            gap = value - kept
            primal = primal + gap * gap
            change = kept if first else kept - jnp.maximum(old - old_sparse_bound, 0.0)
            dual = dual + change * change
            sums_now = (primal, dual)
            if i < rows - 1:
                diff = now[i + 1] - value
            else:
                diff = (near_row - value) * has_below
            old = None if first else old_down[here, spans[i]]
            total, arg, sums_now = shrunk(diff, old, sums_now)
            down_sum[here, spans[i]] = total
            down_arg[here, spans[i]] = arg
            beside = jnp.where(lane == cols - 1, roll(near_right, cols - 1 - i), roll(value, -1))
            diff = (beside - value) * keep_last
            old = None if first else old_right[here, spans[i]]
            total, arg, sums_now = shrunk(diff, old, sums_now)
            right_sum[here, spans[i]] = total
            right_arg[here, spans[i]] = arg
        idle = (jnp.zeros(shape, F32),) * 2
        total, arg, _ = shrunk((now[0] - near_row) * has_above, None if first else old_top[here, :], idle)
        top_sum[here, :] = total
        top_arg[here, :] = arg
        panel = jnp.where(lane < rows, column - near_left, 0.0) * is_panel
        total, arg, _ = shrunk(panel, None if first else old_side[here, :], idle)
        side_sum[here, :] = total
        side_arg[here, :] = arg
        return sums_now

    zero = jnp.zeros(shape, F32)
    body, count = groups(members, step)
    primal, dual = lax.fori_loop(0, count, body, (zero, zero), unroll=UNROLL)
    total, cross, weight = quad[0:GROUP, :], quad[GROUP : 2 * GROUP, :], norm[...]
    if not first:
        total = total + scale * (quad[2 * GROUP : 3 * GROUP, :] + scale * quad[4 * GROUP : 5 * GROUP, :])
        cross = cross + scale * quad[3 * GROUP : 4 * GROUP, :]
    square = total + weight
    share = wide(1.0 / (1.0 + penalty), shape)
    part = wide(penalty / (1.0 + penalty), shape)
    if not last:
        outs[12][...] = weight + part * (2.0 * (cross - weight) + part * square)
    residuals[0:GROUP, :] = primal + share * share * square
    residuals[GROUP : 2 * GROUP, :] = dual


def sides_kernel(rows, cols, first, last, *refs):
    (estimate, sparse, down_sum, right_sum, top_sum, side_sum, down_arg, right_arg, top_arg, side_arg) = refs[:10]
    scalars, projected, fit_gram = refs[10:13]
    at = 13
    if not first:
        other_gram, old_multiplier = refs[13:15]
        at = 15
    rhs_high, rhs_low = refs[at : at + 2]
    if not last:
        side, other_side, multiplier = refs[at + 2 :]
    members = estimate.shape[0]
    shape = (GROUP, cols)
    pixels = rows * cols
    penalty, rescale = scalars[0:1, 0:1], scalars[1:2, 0:1]
    bound = wide(weight_tv / penalty, shape)
    sparse_bound = wide(weight_sparse / penalty, shape)
    scale = wide(rescale, shape)
    weight = wide(penalty, shape)
    share = wide(1.0 / (1.0 + penalty), shape)
    lane = lanes_of(shape)

    def step(base, carry):
        here = pl.ds(base, GROUP)
        arg_above, dual_above = top_arg[here, :], clip(top_sum[here, :], bound)
        arg_left, dual_left = side_arg[here, :], clip(side_sum[here, :], bound)
        for i in range(rows):
            span = slice(i * cols, (i + 1) * cols)
            later = slice(pixels + i * cols, pixels + (i + 1) * cols)
            value = estimate[here, span]
            gram = fit_gram[here, span]
            held = gram
            if not first:
                gram = gram + scale * other_gram[here, span]
                held = gram + scale * old_multiplier[here, span]
            data = (projected[here, span] + weight * held) * share
            dual_data = held - data
            down, dual_down = down_arg[here, span], clip(down_sum[here, span], bound)
            right, dual_right = right_arg[here, span], clip(right_sum[here, span], bound)
            beside = jnp.where(lane == 0, roll(arg_left, -i), roll(right, 1))
            dual_beside = jnp.where(lane == 0, roll(dual_left, -i), roll(dual_right, 1))
            total = sparse[here, span]
            rhs = data + jnp.maximum(total - sparse_bound, 0.0) + prox_tau * value - (
                (arg_above - down) + (beside - right)
            )
            rhs_other = -(
                dual_data
                + jnp.minimum(total, sparse_bound)
                + ((dual_above - dual_down) + (dual_beside - dual_right))
            )
            arg_above, dual_above = down, dual_down
            rhs_high[here, span], rhs_low[here, span] = split(rhs)
            rhs_high[here, later], rhs_low[here, later] = split(rhs_other)
            if not last:
                side[here, span] = rhs
                other_side[here, span] = rhs_other
                multiplier[here, span] = dual_data
        return carry

    body, count = groups(members, step)
    lax.fori_loop(0, count, body, 0, unroll=UNROLL)


def solve_kernel(inv_high, inv_low, rhs_high, rhs_low, fit, other):
    pixels = fit.shape[1]

    def store(start, size, value):
        if start < pixels:
            fit[:, start : start + size] = value
        else:
            other[:, start - pixels : start - pixels + size] = value

    apply_inverse(inv_high, inv_low, rhs_high, rhs_low, store)


def products_kernel(rows, cols, *refs):
    fit, other, side, other_side, multiplier, projected, scalars = refs[:7]
    fit_gram, other_gram, quad, row_edge, left_edge, right_edge = refs[7:]
    members = fit.shape[0]
    shape = (GROUP, cols)
    weight = wide(scalars[0:1, 0:1], shape)
    below = edge_flags()[1]

    def step(base, sums):
        here = pl.ds(base, GROUP)
        aa, ap, ab, bp, bb = sums
        fits, others = [], []
        for i in range(rows):
            span = slice(i * cols, (i + 1) * cols)
            a, b = fit[here, span], other[here, span]
            ga = side[here, span] - SHIFT * a
            gb = other_side[here, span] - SHIFT * b
            fit_gram[here, span] = ga
            other_gram[here, span] = gb
            target = projected[here, span] + weight * multiplier[here, span]
            aa = aa + a * (ga - 2.0 * target)
            ap = ap + a * target
            ab = ab + b * (2.0 * (ga - target))
            bp = bp + b * target
            bb = bb + b * gb
            fits.append(a)
            others.append(b)
        write_edges(base, members, fits, others, below, row_edge, left_edge, right_edge)
        return aa, ap, ab, bp, bb

    zero = jnp.zeros(shape, F32)
    body, count = groups(members, step)
    for index, value in enumerate(lax.fori_loop(0, count, body, (zero,) * 5, unroll=UNROLL)):
        quad[index * GROUP : (index + 1) * GROUP, :] = value


def finish_kernel(rows, cols, fit, other, scalars, sums, abundance):
    members = fit.shape[0]
    rescale = new_penalty(scalars, sums)[2]
    scale = wide(rescale, (members, cols))
    for i in range(rows):
        span = slice(i * cols, (i + 1) * cols)
        abundance[pl.ds(i, members, stride=rows), :] = fit[:, span] + scale * other[:, span]


def flat_swap(value, stride, other_row):
    cols = lax.axis_size("col")
    pairs = []
    for row in range(2):
        for col in range(cols):
            target = (1 - row if other_row else row) * cols + (col ^ stride)
            pairs.append((row * cols + col, target))
    return lax.ppermute(value, ("row", "col"), pairs)


def strides():
    cols = lax.axis_size("col")
    return [1 << bit for bit in reversed(range(cols.bit_length() - 1))]


def regular():
    cols = lax.axis_size("col")
    return lax.axis_size("row") == 2 and cols & (cols - 1) == 0


def total_over_mesh(value):
    if not regular():
        return lax.psum(value, ("row", "col"))
    for stride in strides() + [0]:
        value = value + flat_swap(value, stride, True)
    return value


def shifted(value, axis, step):
    count = lax.axis_size(axis)
    first, last = max(0, -step), min(count, count - step)
    return lax.ppermute(value, axis, [(source, source + step) for source in range(first, last)])


def halos(row_edge, left_edge, right_edge):
    near_row = flat_swap(row_edge, 0, True)
    near_left = shifted(right_edge, "col", 1)
    near_right = shifted(left_edge, "col", -1)
    return near_row, near_left, near_right


def gathered(library):
    half_rows = library.shape[0] // 2
    if not regular() or half_rows % 16 or lax.axis_size("col") < 2:
        return [lax.all_gather(library, "col", axis=0, tiled=True)], True
    parity = lax.axis_index("row")
    bits = lax.axis_index("col")
    for _ in strides():
        parity = parity ^ (bits & 1)
        bits = bits >> 1
    mine = lax.dynamic_slice_in_dim(library, parity * half_rows, half_rows, 0)
    tag = mine
    order = strides()
    reach = [0]
    for stride in order[:-1]:
        got = flat_swap(mine, stride, True)
        mine = jnp.concatenate([mine, got], axis=0)
        reach = reach + [r ^ stride for r in reach]
    rest = flat_swap(mine, order[-1], True)
    reach = reach + [r ^ order[-1] for r in reach]
    other = flat_swap(mine, 0, True)
    other_rest = flat_swap(rest, 0, True)
    return [mine, rest, other, other_rest, tag], reach


def iterate(observed, library):
    channels, rows, cols = observed.shape
    members = library.shape[1]
    pixels = rows * cols
    field = ((members, pixels), F32)
    strip = ((members, cols), F32)
    scalar = ((GROUP, cols), F32)
    pieces, order = gathered(library)
    flat = observed.reshape(channels, pixels)
    columns, row_edge, norm = call(
        functools.partial(survey_kernel, rows, cols),
        [((2 * rows, channels), BF16), ((channels, cols), BF16), scalar],
        [flat],
        flops=2 * rows * channels * pixels,
    )
    near = halos(row_edge, columns, columns)
    half = ((members, members), BF16)
    extended = pltpu.VMEM((members, pixels + 2 * cols), BF16)
    scratch = [
        pltpu.VMEM((members, members), F32),
        pltpu.VMEM((members, members), F32),
        extended,
        extended,
        pltpu.SMEM((2,), F32),
        pltpu.VMEM((cols, channels), BF16),
    ]
    if order is not True:
        scratch.append(pltpu.VMEM((channels, members), BF16))
    work = 2 * members * members * pixels
    projected, inv_high, inv_low, fit, fit_gram, quad, *near = call(
        functools.partial(start_kernel, rows, cols, order),
        [field, half, half, field, field, ((2 * GROUP, cols), F32), strip, strip, strip],
        [flat, *near, *pieces],
        scratch,
        flops=8 * work,
    )
    state = None
    other = other_gram = multiplier = scalars = sums = None
    for iteration in range(ITERS):
        first = iteration == 0
        last = iteration == ITERS - 1
        if first:
            args = [fit, quad, norm, *near]
        else:
            args = [fit, other, quad, norm, *near, scalars, sums, *state[1:6]]
        results = call(
            functools.partial(shrink_kernel, rows, cols, first, last),
            [field] * 4 + [strip] * 2 + [field] * 2 + [strip] * 2
            + [((2 * GROUP, cols), F32), scalar] + ([] if last else [scalar]),
            args,
            flops=work,
        )
        state, residuals, scalars = results[:10], results[10], results[11]
        sums = total_over_mesh(residuals)
        args = [*state, scalars, projected, fit_gram]
        if not first:
            args += [other_gram, multiplier]
        wide_half = ((members, 2 * pixels), BF16)
        rhs_high, rhs_low, *sides = call(
            functools.partial(sides_kernel, rows, cols, first, last),
            [wide_half] * 2 + ([] if last else [field] * 3),
            args,
            flops=2 * work,
        )
        fit, other = call(
            solve_kernel, [field] * 2, [inv_high, inv_low, rhs_high, rhs_low], flops=2 * work
        )
        if last:
            break
        multiplier = sides[2]
        fit_gram, other_gram, quad, *edge = call(
            functools.partial(products_kernel, rows, cols),
            [field] * 2 + [((5 * GROUP, cols), F32), ((2 * members, cols), F32), strip, strip],
            [fit, other, *sides, projected, scalars],
            flops=2 * work,
        )
        near = halos(*edge)
        norm = results[12]
    (abundance,) = call(
        functools.partial(finish_kernel, rows, cols),
        [((members * rows, cols), F32)],
        [fit, other, scalars, sums],
        flops=work // 8,
    )
    return abundance.reshape(members, rows, cols)


def solution(mesh):
    return jax.shard_map(
        iterate,
        mesh=mesh,
        in_specs=(P(None, "row", "col"), P("col", None)),
        out_specs=P(None, "row", "col"),
        check_vma=False,
    )
```

profile of v0, /device:TPU:0, one launch (start us, length us, event | category | flops | bytes accessed | tf_op | source)
XLA Modules:
  0.0 114.2 jit_solution(16510143840121620407)
XLA Ops:
  0.8 3.5 %collective-permute-start.3 = (bf16[32,256]{1,0:T(8,128)(2,1)S(1)}, bf16[32,256]{1,0:T(8,128)(2,1)S(1)}, u32[]{:S(2)}, u32[]{:S(2)}) collective-permute-start(bf16[32,256]{1,0:T(8,128)(2,1)S(1)} %constant_dynamic-slice_fusion.refs_8_), channel_id=1, source_target_pairs={{0,24},{1,25},{2,26},{3,27},{4,28},{5,29},{6,30},{7,31},{8,16},{9,... | collective-permute-start | bytes 49160 | tf_op jit(solution)/shard_map/ppermute | solution.py:511
  5.7 1.9 %collective-permute-start.4 = (bf16[64,256]{1,0:T(8,128)(2,1)S(1)}, bf16[64,256]{1,0:T(8,128)(2,1)S(1)}, u32[]{:S(2)}, u32[]{:S(2)}) collective-permute-start(bf16[64,256]{1,0:T(8,128)(2,1)S(1)} %pad_maximum_fusion.2), channel_id=1, source_target_pairs={{0,20},{1,21},{2,22},{3,23},{4,16},{5,17},{6,18},{7,19},{8,28},{9,... | collective-permute-start | bytes 98312 | tf_op jit(solution)/shard_map/ppermute | solution.py:511
  9.2 1.7 %collective-permute-start.5 = (bf16[128,256]{1,0:T(8,128)(2,1)S(1)}, bf16[128,256]{1,0:T(8,128)(2,1)S(1)}, u32[]{:S(2)}, u32[]{:S(2)}) collective-permute-start(bf16[128,256]{1,0:T(8,128)(2,1)S(1)} %pad_maximum_fusion.1), channel_id=1, source_target_pairs={{0,18},{1,19},{2,16},{3,17},{4,22},{5,23},{6,20},{7,21},{8,26},{9,... | collective-permute-start | bytes 196616 | tf_op jit(solution)/shard_map/ppermute | solution.py:511
  10.9 2.2 %copy.5 = bf16[128,8,8,128]{3,1,2,0:T(8,128)(2,1)S(1)} copy(bf16[128,8,8,128]{3,2,1,0:T(8,128)(2,1)} %bitcast.7) | data formatting | bytes 4194304
  16.5 3.9 %collective-permute-done.6.refs_5_ = bf16[256,256]{1,0:T(8,128)(2,1)S(1)} collective-permute-done((bf16[256,256]{1,0:T(8,128)(2,1)S(1)}, bf16[256,256]{1,0:T(8,128)(2,1)S(1)}, u32[]{:S(2)}, u32[]{:S(2)}) %collective-permute-start.6) | collective-permute-done | bytes 131104 | tf_op jit(solution)/shard_map/ppermute | solution.py:511
  21.8 4.5 %collective-permute-start.1 = (bf16[16,1024]{1,0:T(8,128)(2,1)S(1)}, bf16[16,1024]{1,0:T(8,128)(2,1)S(1)}, u32[]{:S(2)}, u32[]{:S(2)}) collective-permute-start(bf16[16,1024]{1,0:T(8,128)(2,1)S(1)} %get-tuple-element.86), channel_id=1, source_target_pairs={{0,1},{1,2},{2,3},{3,4},{4,5},{5,6},{6,7},{7,8},{8,9},{9,10},{10,1... | collective-permute-start | bytes 98312 | tf_op jit(solution)/shard_map/ppermute | solution.py:535
  28.0 6.9 %shard_map.29 = (f32[256,1024]{1,0:T(8,128)S(1)}, bf16[256,256]{1,0:T(8,128)(2,1)S(1)}, bf16[256,256]{1,0:T(8,128)(2,1)S(1)}, f32[256,1024]{1,0:T(8,128)S(1)}, f...) custom-call(bf16[1024,1024]{1,0:T(8,128)(2,1)S(1)} %bitcast.6, ...), custom_call_target="tpu_custom_call" | custom-call | flops 1073741824 | tf_op jit(solution)/shard_map/pallas_call | solution.py:45
  40.0 4.3 %collective-permute-start.10 = (f32[256,128]{1,0:T(8,128)S(1)}, f32[256,128]{1,0:T(8,128)S(1)}, u32[]{:S(2)}, u32[]{:S(2)}) collective-permute-start(f32[256,128]{1,0:T(8,128)S(1)} %get-tuple-element.118), channel_id=1, source_target_pairs={{0,1},{1,2},{2,3},{3,4},{4,5},{5,6},{6,7},{7,8},{8,9},{9,10},{10,1... | collective-permute-start | bytes 393224 | tf_op jit(solution)/shard_map/ppermute | solution.py:535
  45.6 7.6 %collective-permute-start.12 = (f32[16,128]{1,0:T(8,128)S(1)}, f32[16,128]{1,0:T(8,128)S(1)}, u32[]{:S(2)}, u32[]{:S(2)}) collective-permute-start(f32[16,128]{1,0:T(8,128)S(1)} %get-tuple-element.120), channel_id=1, source_target_pairs={{0,24},{1,25},{2,26},{3,27},{4,28},{5,29},{6,30},{7,31},{8,16},{9,... | collective-permute-start | bytes 24584 | tf_op jit(solution)/shard_map/ppermute | solution.py:511
  53.2 3.4 %collective-permute-done.12 = f32[16,128]{1,0:T(8,128)S(1)} collective-permute-done((f32[16,128]{1,0:T(8,128)S(1)}, f32[16,128]{1,0:T(8,128)S(1)}, u32[]{:S(2)}, u32[]{:S(2)}) %collective-permute-start.12) | collective-permute-done | bytes 8224 | tf_op jit(solution)/shard_map/ppermute | solution.py:511
  56.5 1.9 %collective-permute-start.13 = (f32[16,128]{1,0:T(8,128)S(1)}, f32[16,128]{1,0:T(8,128)S(1)}, u32[]{:S(2)}, u32[]{:S(2)}) collective-permute-start(f32[16,128]{1,0:T(8,128)S(1)} %add.49), channel_id=1, source_target_pairs={{0,20},{1,21},{2,22},{3,23},{4,16},{5,17},{6,18},{7,19},{8,28},{9,... | collective-permute-start | bytes 24584 | tf_op jit(solution)/shard_map/ppermute | solution.py:511
  59.8 3.1 %collective-permute-done.14 = f32[16,128]{1,0:T(8,128)S(1)} collective-permute-done((f32[16,128]{1,0:T(8,128)S(1)}, f32[16,128]{1,0:T(8,128)S(1)}, u32[]{:S(2)}, u32[]{:S(2)}) %collective-permute-start.14) | collective-permute-done | bytes 8224 | tf_op jit(solution)/shard_map/ppermute | solution.py:511
  62.9 3.1 %collective-permute-done.15 = f32[16,128]{1,0:T(8,128)S(1)} collective-permute-done((f32[16,128]{1,0:T(8,128)S(1)}, f32[16,128]{1,0:T(8,128)S(1)}, u32[]{:S(2)}, u32[]{:S(2)}) %collective-permute-start.15) | collective-permute-done | bytes 8224 | tf_op jit(solution)/shard_map/ppermute | solution.py:511
  67.2 2.3 %shard_map.34 = (f32[256,1024]{1,0:T(8,128)S(1)}, f32[256,1024]{1,0:T(8,128)S(1)}, f32[256,1024]{1,0:T(8,128)S(1)}, f32[256,1024]{1,0:T(8,128)S(1)}, f32[256,128...) custom-call(f32[256,1024]{1,0:T(8,128)S(1)} %get-tuple-element.110.r, ...), custom_call_target="tpu_custom_call" | custom-call | flops 134217728 | tf_op jit(solution)/shard_map/pallas_call | solution.py:45
  73.7 2.0 %collective-permute-start.18 = (f32[256,128]{1,0:T(8,128)S(1)}, f32[256,128]{1,0:T(8,128)S(1)}, u32[]{:S(2)}, u32[]{:S(2)}) collective-permute-start(f32[256,128]{1,0:T(8,128)S(1)} %get-tuple-element.144), channel_id=1, source_target_pairs={{0,1},{1,2},{2,3},{3,4},{4,5},{5,6},{6,7},{7,8},{8,9},{9,10},{10,1... | collective-permute-start | bytes 393224 | tf_op jit(solution)/shard_map/ppermute | solution.py:535
  77.2 4.5 %collective-permute-start.20 = (f32[16,128]{1,0:T(8,128)S(1)}, f32[16,128]{1,0:T(8,128)S(1)}, u32[]{:S(2)}, u32[]{:S(2)}) collective-permute-start(f32[16,128]{1,0:T(8,128)S(1)} %get-tuple-element.146), channel_id=1, source_target_pairs={{0,24},{1,25},{2,26},{3,27},{4,28},{5,29},{6,30},{7,31},{8,16},{9,... | collective-permute-start | bytes 24584 | tf_op jit(solution)/shard_map/ppermute | solution.py:511
  81.7 3.0 %collective-permute-done.20 = f32[16,128]{1,0:T(8,128)S(1)} collective-permute-done((f32[16,128]{1,0:T(8,128)S(1)}, f32[16,128]{1,0:T(8,128)S(1)}, u32[]{:S(2)}, u32[]{:S(2)}) %collective-permute-start.20) | collective-permute-done | bytes 8224 | tf_op jit(solution)/shard_map/ppermute | solution.py:511
  84.7 2.3 %collective-permute-start.21 = (f32[16,128]{1,0:T(8,128)S(1)}, f32[16,128]{1,0:T(8,128)S(1)}, u32[]{:S(2)}, u32[]{:S(2)}) collective-permute-start(f32[16,128]{1,0:T(8,128)S(1)} %add.54), channel_id=1, source_target_pairs={{0,20},{1,21},{2,22},{3,23},{4,16},{5,17},{6,18},{7,19},{8,28},{9,... | collective-permute-start | bytes 24584 | tf_op jit(solution)/shard_map/ppermute | solution.py:511
  88.4 3.1 %collective-permute-done.22 = f32[16,128]{1,0:T(8,128)S(1)} collective-permute-done((f32[16,128]{1,0:T(8,128)S(1)}, f32[16,128]{1,0:T(8,128)S(1)}, u32[]{:S(2)}, u32[]{:S(2)}) %collective-permute-start.22) | collective-permute-done | bytes 8224 | tf_op jit(solution)/shard_map/ppermute | solution.py:511
  91.4 3.1 %collective-permute-done.23 = f32[16,128]{1,0:T(8,128)S(1)} collective-permute-done((f32[16,128]{1,0:T(8,128)S(1)}, f32[16,128]{1,0:T(8,128)S(1)}, u32[]{:S(2)}, u32[]{:S(2)}) %collective-permute-start.23) | collective-permute-done | bytes 8224 | tf_op jit(solution)/shard_map/ppermute | solution.py:511
  95.8 2.2 %shard_map.38 = (f32[256,1024]{1,0:T(8,128)S(1)}, f32[256,1024]{1,0:T(8,128)S(1)}, f32[256,1024]{1,0:T(8,128)S(1)}, f32[256,1024]{1,0:T(8,128)S(1)}, f32[256,128...) custom-call(f32[256,1024]{1,0:T(8,128)S(1)} %get-tuple-element.136.r, ...), custom_call_target="tpu_custom_call" | custom-call | flops 134217728 | tf_op jit(solution)/shard_map/pallas_call | solution.py:45
  98.8 3.2 %collective-permute-done.25 = f32[16,128]{1,0:T(8,128)S(1)} collective-permute-done((f32[16,128]{1,0:T(8,128)S(1)}, f32[16,128]{1,0:T(8,128)S(1)}, u32[]{:S(2)}, u32[]{:S(2)}) %collective-permute-start.25) | collective-permute-done | bytes 8224 | tf_op jit(solution)/shard_map/ppermute | solution.py:511
  102.1 1.7 %collective-permute-start.26 = (f32[16,128]{1,0:T(8,128)S(1)}, f32[16,128]{1,0:T(8,128)S(1)}, u32[]{:S(2)}, u32[]{:S(2)}) collective-permute-start(f32[16,128]{1,0:T(8,128)S(1)} %add.59), channel_id=1, source_target_pairs={{0,20},{1,21},{2,22},{3,23},{4,16},{5,17},{6,18},{7,19},{8,28},{9,... | collective-permute-start | bytes 24584 | tf_op jit(solution)/shard_map/ppermute | solution.py:511
  105.2 3.1 %collective-permute-done.27 = f32[16,128]{1,0:T(8,128)S(1)} collective-permute-done((f32[16,128]{1,0:T(8,128)S(1)}, f32[16,128]{1,0:T(8,128)S(1)}, u32[]{:S(2)}, u32[]{:S(2)}) %collective-permute-start.27) | collective-permute-done | bytes 8224 | tf_op jit(solution)/shard_map/ppermute | solution.py:511
  (72 shorter events, 35.5 us)
Async XLA Ops:
  0.8 4.9 %collective-permute-start.3 = (bf16[32,256]{1,0:T(8,128)(2,1)S(1)}, bf16[32,256]{1,0:T(8,128)(2,1)S(1)}, u32[]{:S(2)}, u32[]{:S(2)}) collective-permute-start(bf16[32,256]{1,0:T(8,128)(2,1)S(1)} %constant_dynamic-slice_fusion.refs_8_), channel_id=1, source_target_pairs={{0,24},{1,25},{2,26},{3,27},{4,28},{5,29},{6,30},{7,31},{8,16},{9,... | collective-permute-start | bytes 49160 | tf_op jit(solution)/shard_map/ppermute | solution.py:511
  5.7 3.5 %collective-permute-start.4 = (bf16[64,256]{1,0:T(8,128)(2,1)S(1)}, bf16[64,256]{1,0:T(8,128)(2,1)S(1)}, u32[]{:S(2)}, u32[]{:S(2)}) collective-permute-start(bf16[64,256]{1,0:T(8,128)(2,1)S(1)} %pad_maximum_fusion.2), channel_id=1, source_target_pairs={{0,20},{1,21},{2,22},{3,23},{4,16},{5,17},{6,18},{7,19},{8,28},{9,... | collective-permute-start | bytes 98312 | tf_op jit(solution)/shard_map/ppermute | solution.py:511
  9.2 5.6 %collective-permute-start.5 = (bf16[128,256]{1,0:T(8,128)(2,1)S(1)}, bf16[128,256]{1,0:T(8,128)(2,1)S(1)}, u32[]{:S(2)}, u32[]{:S(2)}) collective-permute-start(bf16[128,256]{1,0:T(8,128)(2,1)S(1)} %pad_maximum_fusion.1), channel_id=1, source_target_pairs={{0,18},{1,19},{2,16},{3,17},{4,22},{5,23},{6,20},{7,21},{8,26},{9,... | collective-permute-start | bytes 196616 | tf_op jit(solution)/shard_map/ppermute | solution.py:511
  14.3 13.7 %collective-permute-start = (bf16[1024,128]{1,0:T(8,128)(2,1)S(1)}, bf16[1024,128]{1,0:T(8,128)(2,1)S(1)}, u32[]{:S(2)}, u32[]{:S(2)}) collective-permute-start(bf16[1024,128]{1,0:T(8,128)(2,1)S(1)} %get-tuple-element.85), channel_id=1, source_target_pairs={{0,16},{1,17},{2,18},{3,19},{4,20},{5,21},{6,22},{7,23},{8,24},{9,... | collective-permute-start | bytes 786440 | tf_op jit(solution)/shard_map/ppermute | solution.py:511
  14.8 5.6 %collective-permute-start.6 = (bf16[256,256]{1,0:T(8,128)(2,1)S(1)}, bf16[256,256]{1,0:T(8,128)(2,1)S(1)}, u32[]{:S(2)}, u32[]{:S(2)}) collective-permute-start(bf16[256,256]{1,0:T(8,128)(2,1)S(1)} %pad_maximum_fusion.refs_4_), channel_id=1, source_target_pairs={{0,17},{1,16},{2,19},{3,18},{4,21},{5,20},{6,23},{7,22},{8,25},{9,... | collective-permute-start | bytes 393224 | tf_op jit(solution)/shard_map/ppermute | solution.py:511
  16.0 11.9 %collective-permute-start.7 = (bf16[256,256]{1,0:T(8,128)(2,1)S(1)}, bf16[256,256]{1,0:T(8,128)(2,1)S(1)}, u32[]{:S(2)}, u32[]{:S(2)}) collective-permute-start(bf16[256,256]{1,0:T(8,128)(2,1)S(1)} %pad_maximum_fusion.refs_4_), channel_id=1, source_target_pairs={{0,16},{1,17},{2,18},{3,19},{4,20},{5,21},{6,22},{7,23},{8,24},{9,... | collective-permute-start | bytes 393224 | tf_op jit(solution)/shard_map/ppermute | solution.py:511
  20.4 7.5 %collective-permute-start.8 = (bf16[256,256]{1,0:T(8,128)(2,1)S(1)}, bf16[256,256]{1,0:T(8,128)(2,1)S(1)}, u32[]{:S(2)}, u32[]{:S(2)}) collective-permute-start(bf16[256,256]{1,0:T(8,128)(2,1)S(1)} %collective-permute-done.6.refs_5_), channel_id=1, source_target_pairs={{0,16},{1,17},{2,18},{3,19},{4,20},{5,21},{6,22},{7,23},{8,24},{9,... | collective-permute-start | bytes 393224 | tf_op jit(solution)/shard_map/ppermute | solution.py:511
  20.6 5.8 %collective-permute-start.2 = (bf16[16,1024]{1,0:T(8,128)(2,1)S(1)}, bf16[16,1024]{1,0:T(8,128)(2,1)S(1)}, u32[]{:S(2)}, u32[]{:S(2)}) collective-permute-start(bf16[16,1024]{1,0:T(8,128)(2,1)S(1)} %get-tuple-element.86), channel_id=1, source_target_pairs={{1,0},{2,1},{3,2},{4,3},{5,4},{6,5},{7,6},{8,7},{9,8},{10,9},{11,1... | collective-permute-start | bytes 98312 | tf_op jit(solution)/shard_map/ppermute | solution.py:535
  21.8 6.1 %collective-permute-start.1 = (bf16[16,1024]{1,0:T(8,128)(2,1)S(1)}, bf16[16,1024]{1,0:T(8,128)(2,1)S(1)}, u32[]{:S(2)}, u32[]{:S(2)}) collective-permute-start(bf16[16,1024]{1,0:T(8,128)(2,1)S(1)} %get-tuple-element.86), channel_id=1, source_target_pairs={{0,1},{1,2},{2,3},{3,4},{4,5},{5,6},{6,7},{7,8},{8,9},{9,10},{10,1... | collective-permute-start | bytes 98312 | tf_op jit(solution)/shard_map/ppermute | solution.py:535
  39.9 27.3 %collective-permute-start.9 = (f32[512,128]{1,0:T(8,128)S(1)}, f32[512,128]{1,0:T(8,128)S(1)}, u32[]{:S(2)}, u32[]{:S(2)}) collective-permute-start(f32[512,128]{1,0:T(8,128)S(1)} %get-tuple-element.117), channel_id=1, source_target_pairs={{0,16},{1,17},{2,18},{3,19},{4,20},{5,21},{6,22},{7,23},{8,24},{9,... | collective-permute-start | bytes 786440 | tf_op jit(solution)/shard_map/ppermute | solution.py:511
  40.0 27.2 %collective-permute-start.10 = (f32[256,128]{1,0:T(8,128)S(1)}, f32[256,128]{1,0:T(8,128)S(1)}, u32[]{:S(2)}, u32[]{:S(2)}) collective-permute-start(f32[256,128]{1,0:T(8,128)S(1)} %get-tuple-element.118), channel_id=1, source_target_pairs={{0,1},{1,2},{2,3},{3,4},{4,5},{5,6},{6,7},{7,8},{8,9},{9,10},{10,1... | collective-permute-start | bytes 393224 | tf_op jit(solution)/shard_map/ppermute | solution.py:535
  44.3 22.9 %collective-permute-start.11 = (f32[256,128]{1,0:T(8,128)S(1)}, f32[256,128]{1,0:T(8,128)S(1)}, u32[]{:S(2)}, u32[]{:S(2)}) collective-permute-start(f32[256,128]{1,0:T(8,128)S(1)} %get-tuple-element.119), channel_id=1, source_target_pairs={{1,0},{2,1},{3,2},{4,3},{5,4},{6,5},{7,6},{8,7},{9,8},{10,9},{11,1... | collective-permute-start | bytes 393224 | tf_op jit(solution)/shard_map/ppermute | solution.py:535
  45.6 11.0 %collective-permute-start.12 = (f32[16,128]{1,0:T(8,128)S(1)}, f32[16,128]{1,0:T(8,128)S(1)}, u32[]{:S(2)}, u32[]{:S(2)}) collective-permute-start(f32[16,128]{1,0:T(8,128)S(1)} %get-tuple-element.120), channel_id=1, source_target_pairs={{0,24},{1,25},{2,26},{3,27},{4,28},{5,29},{6,30},{7,31},{8,16},{9,... | collective-permute-start | bytes 24584 | tf_op jit(solution)/shard_map/ppermute | solution.py:511
  56.5 3.3 %collective-permute-start.13 = (f32[16,128]{1,0:T(8,128)S(1)}, f32[16,128]{1,0:T(8,128)S(1)}, u32[]{:S(2)}, u32[]{:S(2)}) collective-permute-start(f32[16,128]{1,0:T(8,128)S(1)} %add.49), channel_id=1, source_target_pairs={{0,20},{1,21},{2,22},{3,23},{4,16},{5,17},{6,18},{7,19},{8,28},{9,... | collective-permute-start | bytes 24584 | tf_op jit(solution)/shard_map/ppermute | solution.py:511
  62.9 3.1 %collective-permute-start.15 = (f32[16,128]{1,0:T(8,128)S(1)}, f32[16,128]{1,0:T(8,128)S(1)}, u32[]{:S(2)}, u32[]{:S(2)}) collective-permute-start(f32[16,128]{1,0:T(8,128)S(1)} %add.51), channel_id=1, source_target_pairs={{0,17},{1,16},{2,19},{3,18},{4,21},{5,20},{6,23},{7,22},{8,25},{9,... | collective-permute-start | bytes 24584 | tf_op jit(solution)/shard_map/ppermute | solution.py:511
  73.3 22.5 %collective-permute-start.17 = (f32[512,128]{1,0:T(8,128)S(1)}, f32[512,128]{1,0:T(8,128)S(1)}, u32[]{:S(2)}, u32[]{:S(2)}) collective-permute-start(f32[512,128]{1,0:T(8,128)S(1)} %get-tuple-element.143), channel_id=1, source_target_pairs={{0,16},{1,17},{2,18},{3,19},{4,20},{5,21},{6,22},{7,23},{8,24},{9,... | collective-permute-start | bytes 786440 | tf_op jit(solution)/shard_map/ppermute | solution.py:511
  73.7 22.0 %collective-permute-start.18 = (f32[256,128]{1,0:T(8,128)S(1)}, f32[256,128]{1,0:T(8,128)S(1)}, u32[]{:S(2)}, u32[]{:S(2)}) collective-permute-start(f32[256,128]{1,0:T(8,128)S(1)} %get-tuple-element.144), channel_id=1, source_target_pairs={{0,1},{1,2},{2,3},{3,4},{4,5},{5,6},{6,7},{7,8},{8,9},{9,10},{10,1... | collective-permute-start | bytes 393224 | tf_op jit(solution)/shard_map/ppermute | solution.py:535
  75.7 20.0 %collective-permute-start.19 = (f32[256,128]{1,0:T(8,128)S(1)}, f32[256,128]{1,0:T(8,128)S(1)}, u32[]{:S(2)}, u32[]{:S(2)}) collective-permute-start(f32[256,128]{1,0:T(8,128)S(1)} %get-tuple-element.145), channel_id=1, source_target_pairs={{1,0},{2,1},{3,2},{4,3},{5,4},{6,5},{7,6},{8,7},{9,8},{10,9},{11,1... | collective-permute-start | bytes 393224 | tf_op jit(solution)/shard_map/ppermute | solution.py:535
  77.2 7.5 %collective-permute-start.20 = (f32[16,128]{1,0:T(8,128)S(1)}, f32[16,128]{1,0:T(8,128)S(1)}, u32[]{:S(2)}, u32[]{:S(2)}) collective-permute-start(f32[16,128]{1,0:T(8,128)S(1)} %get-tuple-element.146), channel_id=1, source_target_pairs={{0,24},{1,25},{2,26},{3,27},{4,28},{5,29},{6,30},{7,31},{8,16},{9,... | collective-permute-start | bytes 24584 | tf_op jit(solution)/shard_map/ppermute | solution.py:511
  84.7 3.6 %collective-permute-start.21 = (f32[16,128]{1,0:T(8,128)S(1)}, f32[16,128]{1,0:T(8,128)S(1)}, u32[]{:S(2)}, u32[]{:S(2)}) collective-permute-start(f32[16,128]{1,0:T(8,128)S(1)} %add.54), channel_id=1, source_target_pairs={{0,20},{1,21},{2,22},{3,23},{4,16},{5,17},{6,18},{7,19},{8,28},{9,... | collective-permute-start | bytes 24584 | tf_op jit(solution)/shard_map/ppermute | solution.py:511
  88.4 3.1 %collective-permute-start.22 = (f32[16,128]{1,0:T(8,128)S(1)}, f32[16,128]{1,0:T(8,128)S(1)}, u32[]{:S(2)}, u32[]{:S(2)}) collective-permute-start(f32[16,128]{1,0:T(8,128)S(1)} %add.55), channel_id=1, source_target_pairs={{0,18},{1,19},{2,16},{3,17},{4,22},{5,23},{6,20},{7,21},{8,26},{9,... | collective-permute-start | bytes 24584 | tf_op jit(solution)/shard_map/ppermute | solution.py:511
  91.4 3.1 %collective-permute-start.23 = (f32[16,128]{1,0:T(8,128)S(1)}, f32[16,128]{1,0:T(8,128)S(1)}, u32[]{:S(2)}, u32[]{:S(2)}) collective-permute-start(f32[16,128]{1,0:T(8,128)S(1)} %add.56), channel_id=1, source_target_pairs={{0,17},{1,16},{2,19},{3,18},{4,21},{5,20},{6,23},{7,22},{8,25},{9,... | collective-permute-start | bytes 24584 | tf_op jit(solution)/shard_map/ppermute | solution.py:511
  98.0 4.0 %collective-permute-start.25 = (f32[16,128]{1,0:T(8,128)S(1)}, f32[16,128]{1,0:T(8,128)S(1)}, u32[]{:S(2)}, u32[]{:S(2)}) collective-permute-start(f32[16,128]{1,0:T(8,128)S(1)} %get-tuple-element.164), channel_id=1, source_target_pairs={{0,24},{1,25},{2,26},{3,27},{4,28},{5,29},{6,30},{7,31},{8,16},{9,... | collective-permute-start | bytes 24584 | tf_op jit(solution)/shard_map/ppermute | solution.py:511
  102.1 3.1 %collective-permute-start.26 = (f32[16,128]{1,0:T(8,128)S(1)}, f32[16,128]{1,0:T(8,128)S(1)}, u32[]{:S(2)}, u32[]{:S(2)}) collective-permute-start(f32[16,128]{1,0:T(8,128)S(1)} %add.59), channel_id=1, source_target_pairs={{0,20},{1,21},{2,22},{3,23},{4,16},{5,17},{6,18},{7,19},{8,28},{9,... | collective-permute-start | bytes 24584 | tf_op jit(solution)/shard_map/ppermute | solution.py:511
  (7 other events, 13.8 us)
where the time goes:
time: 114 us
  starting transfers between devices  44.7 us (39%)
  waiting for transfers between devices  40.9 us (36%)
  Pallas kernels  25.3 us (22%)
  local copies, waits for them, and re-layouts  2.97 us (3%)
    ppermute x24, waiting for transfers between devices, flat_swap(): return lax.ppermute(value, ('row', 'col'), pairs)  39.4 us
    ppermute x24, starting transfers between devices, flat_swap(): return lax.ppermute(value, ('row', 'col'), pairs)  29.8 us
    pallas_call x14, Pallas kernels, call(): pl.pallas_call(body, out_shape=[jax.ShapeDtypeStruct(*out) for out in out...  25.3 us
    ppermute x6, starting transfers between devices, shifted(): lax.ppermute(value, axis, [(source, source + step) for source in range(fi...  14.9 us
    unnamed x3, local copies, waits for them, and re-layouts  2.96 us
  transfers between devices with their start and end apart: 30, of which 18 were waited for; matrix products, arithmetic and copies ran while one was open for 2% of the time, Pallas kernels for 3%

commit v1 on v0

--- a/solution.py
+++ b/solution.py
@@ -6,6 +6,7 @@
 from jax.experimental import pallas as pl
 from jax.experimental.pallas import tpu as pltpu
 from jax.sharding import PartitionSpec as P
+
 
 ITERS = 3
 
@@ -123,39 +124,48 @@
         store(start, block, dot(inv_high[...], high) + (dot(inv_high[...], low) + dot(inv_low[...], high)))
 
 
-def survey_kernel(rows, cols, observed, columns, row_edge, norm):
-    channels, pixels = observed.shape
+def survey_kernel(rows, cols, observed, flat, columns, row_edge, norm, wide_band):
+    channels, pixels = flat.shape
+    tall = 2 * GROUP
+    zero = jnp.zeros((tall, cols), F32)
+
+    def widen(index, total):
+        total = list(total)
+        for part in range(rows):
+            here = pl.ds(pl.multiple_of((index * rows + part) * tall, tall), tall)
+            value = observed[here, :].astype(F32)
+            wide_band[here, :] = value
+            total[part % 2] = total[part % 2] + value * value
+        return tuple(total)
+
+    even, odd = lax.fori_loop(0, channels // tall, widen, (zero, zero), unroll=4)
+    total = even + odd
+    norm[...] = total[:GROUP, :] + total[GROUP:, :]
+
+    def place(index, carry):
+        start = pl.multiple_of(index * tall, tall)
+        for i in range(rows):
+            value = wide_band[pl.ds(start * rows + i, tall, stride=rows), :]
+            flat[pl.ds(start, tall), i * cols : (i + 1) * cols] = value.astype(BF16)
+        return carry
+
+    lax.fori_loop(0, channels // tall, place, 0, unroll=4)
     spot = lax.broadcasted_iota(jnp.int32, (2 * rows, pixels), 0)
     pixel = lax.broadcasted_iota(jnp.int32, (2 * rows, pixels), 1)
     wanted = jnp.where(spot < rows, spot * cols, (spot - rows) * cols + cols - 1)
     chosen = flag(pixel == wanted).astype(BF16)
     columns[...] = lax.dot_general(
-        chosen, observed[...], (((1,), (1,)), ((), ())), preferred_element_type=F32
+        chosen, flat[...], (((1,), (1,)), ((), ())), preferred_element_type=F32
     ).astype(BF16)
     is_upper = edge_flags()[1] > 0.0
 
     @pl.when(is_upper)
     def _():
-        row_edge[...] = observed[:, pixels - cols :]
+        row_edge[...] = flat[:, pixels - cols :]
 
     @pl.when(jnp.logical_not(is_upper))
     def _():
-        row_edge[...] = observed[:, :cols]
-
-    tall = 2 * GROUP
-
-    def step(index, total):
-        here = pl.ds(pl.multiple_of(index * tall, tall), tall)
-        total = list(total)
-        for i in range(rows):
-            value = observed[here, i * cols : (i + 1) * cols].astype(F32)
-            total[i % 2] = total[i % 2] + value * value
-        return tuple(total)
-
-    zero = jnp.zeros((tall, cols), F32)
-    even, odd = lax.fori_loop(0, channels // tall, step, (zero, zero), unroll=8)
-    total = even + odd
-    norm[...] = total[:GROUP, :] + total[GROUP:, :]
+        row_edge[...] = flat[:, :cols]
 
 
 def start_kernel(rows, cols, order, *refs):
@@ -218,20 +228,47 @@
     quad[GROUP : 2 * GROUP, :] = cross
 
 
-def write_edges(base, members, a, b, below, row_edge, left_edge, right_edge):
+def write_edges(base, members, a, b, below, row_edge, panel):
     here = pl.ds(base, GROUP)
     is_upper = below > 0.0
     row_edge[here, :] = jnp.where(is_upper, a[-1], a[0])
     row_edge[pl.ds(base + members, GROUP), :] = jnp.where(is_upper, b[-1], b[0])
     lane = lanes_of(a[0].shape)
     cols = a[0].shape[1]
-    left = jnp.zeros_like(a[0])
-    right = jnp.zeros_like(a[0])
+    count = len(a) + len(b)
+    first = jnp.zeros_like(a[0])
+    final = jnp.zeros_like(a[0])
     for i, value in enumerate(a + b):
-        left = jnp.where(lane == i, roll(value, i), left)
-        right = jnp.where(lane == i, roll(value, i + 1 - cols), right)
-    left_edge[here, :] = left
-    right_edge[here, :] = right
+        turned = roll(value, i)
+        first = jnp.where(lane == i, turned, first)
+        final = jnp.where(lane == (i - 1) % cols, turned, final)
+    panel[here, :] = jnp.where(lane < count, first, roll(final, count + 1))
+
+
+def pack_edges(panel, rows, to_pair, to_next):
+    members, cols = panel.shape
+    count = 2 * rows
+    is_odd = (lax.axis_index("col") & 1) > 0
+    for part in range(members // cols):
+        turned = jnp.transpose(panel[part * cols : (part + 1) * cols, :])
+        first, final = turned[:count, :], turned[count : 2 * count, :]
+        here = slice(part * count, (part + 1) * count)
+        to_pair[here, :] = jnp.where(is_odd, first, final)
+        to_next[here, :] = jnp.where(is_odd, final, first)
+
+
+def unpack_edges(panel, rows, from_pair, skip, from_next):
+    members, cols = panel.shape
+    count = 2 * rows
+    is_odd = (lax.axis_index("col") & 1) > 0
+    rest = jnp.zeros((cols - 2 * count, cols), F32)
+    for part in range(members // cols):
+        pair = from_pair[skip + part * count : skip + (part + 1) * count, :]
+        other = from_next[part * count : (part + 1) * count, :]
+        on_left, on_right = jnp.where(is_odd, pair, other), jnp.where(is_odd, other, pair)
+        panel[part * cols : (part + 1) * cols, :] = jnp.transpose(
+            jnp.concatenate([on_left, on_right, rest], axis=0)
+        )
 
 
 def place_library(pieces, full, order):
@@ -270,9 +307,11 @@
         fit, quad, norm, row_halo, left_halo, right_halo = refs[:6]
         outs = refs[6:]
     else:
-        (fit, other, quad, norm, row_halo, left_halo, right_halo, scalars, sums) = refs[:9]
+        (fit, other, quad, norm, row_halo, from_pair, from_next, scalars, sums) = refs[:9]
         (old_sparse, old_down, old_right, old_top, old_side) = refs[9:14]
         outs = refs[14:]
+        beside = outs[-1]
+        unpack_edges(beside, rows, from_pair, 2 * GROUP, from_next)
     (estimate, sparse, down_sum, right_sum, top_sum, side_sum, down_arg, right_arg, top_arg, side_arg) = outs[:10]
     residuals, new_scalars = outs[10:12]
     members = fit.shape[0]
@@ -322,8 +361,8 @@
         else:
             now = [mixed(fit[here, span], other[here, span]) for span in spans]
             near_row = mixed(row_halo[here, :], row_halo[pl.ds(base + members, GROUP), :])
-            near_left = mixed(left_halo[here, :], roll(left_halo[here, :], -rows))
-            near_right = mixed(right_halo[here, :], roll(right_halo[here, :], -rows))
+            near_left = mixed(beside[here, :], roll(beside[here, :], -rows))
+            near_right = roll(near_left, -2 * rows)
         column = jnp.zeros(shape, F32)
         for i in range(rows):
             value = now[i]
@@ -350,8 +389,8 @@
             total, arg, sums_now = shrunk(diff, old, sums_now)
             down_sum[here, spans[i]] = total
             down_arg[here, spans[i]] = arg
-            beside = jnp.where(lane == cols - 1, roll(near_right, cols - 1 - i), roll(value, -1))
-            diff = (beside - value) * keep_last
+            following = jnp.where(lane == cols - 1, roll(near_right, cols - 1 - i), roll(value, -1))
+            diff = (following - value) * keep_last
             old = None if first else old_right[here, spans[i]]
             total, arg, sums_now = shrunk(diff, old, sums_now)
             right_sum[here, spans[i]] = total
@@ -444,8 +483,14 @@
     lax.fori_loop(0, count, body, 0, unroll=UNROLL)
 
 
-def solve_kernel(inv_high, inv_low, rhs_high, rhs_low, fit, other):
-    pixels = fit.shape[1]
+def solve_kernel(rows, cols, last, *refs):
+    inv_high, inv_low, rhs_high, rhs_low = refs[:4]
+    if last:
+        fit, other = refs[4:]
+    else:
+        side, other_side, multiplier, projected, scalars = refs[4:9]
+        fit, other, fit_gram, other_gram, quad, row_edge, to_pair, to_next, panel = refs[9:]
+    members, pixels = fit.shape
 
     def store(start, size, value):
         if start < pixels:
@@ -454,12 +499,8 @@
             other[:, start - pixels : start - pixels + size] = value
 
     apply_inverse(inv_high, inv_low, rhs_high, rhs_low, store)
-
-
-def products_kernel(rows, cols, *refs):
-    fit, other, side, other_side, multiplier, projected, scalars = refs[:7]
-    fit_gram, other_gram, quad, row_edge, left_edge, right_edge = refs[7:]
-    members = fit.shape[0]
+    if last:
+        return
     shape = (GROUP, cols)
     weight = wide(scalars[0:1, 0:1], shape)
     below = edge_flags()[1]
@@ -483,13 +524,14 @@
             bb = bb + b * gb
             fits.append(a)
             others.append(b)
-        write_edges(base, members, fits, others, below, row_edge, left_edge, right_edge)
+        write_edges(base, members, fits, others, below, row_edge, panel)
         return aa, ap, ab, bp, bb
 
     zero = jnp.zeros(shape, F32)
     body, count = groups(members, step)
     for index, value in enumerate(lax.fori_loop(0, count, body, (zero,) * 5, unroll=UNROLL)):
         quad[index * GROUP : (index + 1) * GROUP, :] = value
+    pack_edges(panel, rows, to_pair, to_next)
 
 
 def finish_kernel(rows, cols, fit, other, scalars, sums, abundance):
@@ -535,11 +577,36 @@
     return lax.ppermute(value, axis, [(source, source + step) for source in range(first, last)])
 
 
-def halos(row_edge, left_edge, right_edge):
+def band_halos(row_edge, columns):
     near_row = flat_swap(row_edge, 0, True)
-    near_left = shifted(right_edge, "col", 1)
-    near_right = shifted(left_edge, "col", -1)
+    near_left = shifted(columns, "col", 1)
+    near_right = shifted(columns, "col", -1)
     return near_row, near_left, near_right
+
+
+def next_swap(value):
+    count = lax.axis_size("col")
+    pairs = []
+    for low in range(1, count - 1, 2):
+        pairs += [(low, low + 1), (low + 1, low)]
+    return lax.ppermute(value, "col", pairs)
+
+
+def sums_and_halos(value, edges):
+    row_edge, to_pair, to_next = edges
+    near_row = flat_swap(row_edge, 0, True)
+    from_next = next_swap(to_next)
+    if not regular():
+        both = jnp.concatenate([value, to_pair], axis=0)
+        pairs = [(c, c ^ 1) for c in range(lax.axis_size("col")) if c ^ 1 < lax.axis_size("col")]
+        return lax.psum(value, ("row", "col")), near_row, lax.ppermute(both, "col", pairs), from_next
+    stages = strides()
+    for stride in stages[:-1]:
+        value = value + flat_swap(value, stride, True)
+    from_pair = flat_swap(jnp.concatenate([value, to_pair], axis=0), stages[-1], False)
+    value = value + from_pair[: value.shape[0], :]
+    value = value + flat_swap(value, 0, True)
+    return value, near_row, from_pair, from_next
 
 
 def gathered(library):
@@ -574,14 +641,14 @@
     strip = ((members, cols), F32)
     scalar = ((GROUP, cols), F32)
     pieces, order = gathered(library)
-    flat = observed.reshape(channels, pixels)
-    columns, row_edge, norm = call(
+    flat, columns, row_edge, norm = call(
         functools.partial(survey_kernel, rows, cols),
-        [((2 * rows, channels), BF16), ((channels, cols), BF16), scalar],
-        [flat],
+        [((channels, pixels), BF16), ((2 * rows, channels), BF16), ((channels, cols), BF16), scalar],
+        [observed.reshape(channels * rows, cols)],
+        [pltpu.VMEM((channels * rows, cols), F32)],
         flops=2 * rows * channels * pixels,
     )
-    near = halos(row_edge, columns, columns)
+    near = band_halos(row_edge, columns)
     half = ((members, members), BF16)
     extended = pltpu.VMEM((members, pixels + 2 * cols), BF16)
     scratch = [
@@ -616,10 +683,12 @@
             [field] * 4 + [strip] * 2 + [field] * 2 + [strip] * 2
             + [((2 * GROUP, cols), F32), scalar] + ([] if last else [scalar]),
             args,
+            [] if first else [pltpu.VMEM(*strip)],
             flops=work,
         )
         state, residuals, scalars = results[:10], results[10], results[11]
-        sums = total_over_mesh(residuals)
+        if last:
+            sums = total_over_mesh(residuals)
         args = [*state, scalars, projected, fit_gram]
         if not first:
             args += [other_gram, multiplier]
@@ -630,19 +699,25 @@
             args,
             flops=2 * work,
         )
-        fit, other = call(
-            solve_kernel, [field] * 2, [inv_high, inv_low, rhs_high, rhs_low], flops=2 * work
+        packed = ((2 * rows * members // cols, cols), F32)
+        if last:
+            outs, more = [], []
+        else:
+            multiplier = sides[2]
+            outs = [field] * 2 + [((5 * GROUP, cols), F32), ((2 * members, cols), F32), packed, packed]
+            more = [*sides, projected, scalars]
+        results_of = call(
+            functools.partial(solve_kernel, rows, cols, last),
+            [field] * 2 + outs,
+            [inv_high, inv_low, rhs_high, rhs_low, *more],
+            [] if last else [pltpu.VMEM(*strip)],
+            flops=2 * work,
         )
+        fit, other = results_of[:2]
         if last:
             break
-        multiplier = sides[2]
-        fit_gram, other_gram, quad, *edge = call(
-            functools.partial(products_kernel, rows, cols),
-            [field] * 2 + [((5 * GROUP, cols), F32), ((2 * members, cols), F32), strip, strip],
-            [fit, other, *sides, projected, scalars],
-            flops=2 * work,
-        )
-        near = halos(*edge)
+        fit_gram, other_gram, quad, *edge = results_of[2:]
+        sums, *near = sums_and_halos(residuals, edge)
         norm = results[12]
     (abundance,) = call(
         functools.partial(finish_kernel, rows, cols),

time: 114 us -> 100 us (0.88)
  waiting for transfers between devices: 40.9 us -> 23.6 us
  Pallas kernels: 25.3 us -> 28 us
  starting transfers between devices: 44.7 us -> 45.9 us
    ppermute x24, waiting for transfers between devices: 39.4 us -> 22 us  [flat_swap(): return lax.ppermute(value, ('row', 'col'), pairs)]
    ppermute x6 -> x2, starting transfers between devices: 14.9 us -> 5.83 us  [shifted(): lax.ppermute(value, axis, [(source, source + step) for source in range(fi...]
    ppermute x24, starting transfers between devices: 29.8 us -> 38.6 us  [flat_swap(): return lax.ppermute(value, ('row', 'col'), pairs)]
    pallas_call x14 -> x12, Pallas kernels: 25.3 us -> 28 us  [call(): pl.pallas_call(body, out_shape=[jax.ShapeDtypeStruct(*out) for out in out...]
    ppermute x0 -> x2, starting transfers between devices: none -> 1.49 us  [next_swap(): return lax.ppermute(value, 'col', pairs)]
    unnamed x3 -> x4, local copies, waits for them, and re-layouts: 2.96 us -> 2.35 us
  transfers between devices with their start and end apart: 30 -> 28, of which waited for: 18 -> 14; matrix products, arithmetic and copies ran while one was open for 2% -> 0% of each run, Pallas kernels for 3% -> 14%
where the time goes in v1:
time: 100 us
  starting transfers between devices  45.9 us (46%)
  Pallas kernels  28 us (28%)
  waiting for transfers between devices  23.6 us (24%)
  local copies, waits for them, and re-layouts  2.35 us (2%)
    ppermute x24, starting transfers between devices, flat_swap(): return lax.ppermute(value, ('row', 'col'), pairs)  38.6 us
    pallas_call x12, Pallas kernels, call(): pl.pallas_call(body, out_shape=[jax.ShapeDtypeStruct(*out) for out in out...  28 us
    ppermute x24, waiting for transfers between devices, flat_swap(): return lax.ppermute(value, ('row', 'col'), pairs)  22 us
    ppermute x2, starting transfers between devices, shifted(): lax.ppermute(value, axis, [(source, source + step) for source in range(fi...  5.83 us
    unnamed x4, local copies, waits for them, and re-layouts  2.35 us
  transfers between devices with their start and end apart: 28, of which 14 were waited for; matrix products, arithmetic and copies ran while one was open for 0% of the time, Pallas kernels for 14%

profile of v1, /device:TPU:0, one launch (start us, length us, event | category | flops | bytes accessed | tf_op | source)
XLA Modules:
  0.0 100.1 jit_solution(5512785046480265654)
XLA Ops:
  0.8 3.5 %collective-permute-start.3 = (bf16[32,256]{1,0:T(8,128)(2,1)S(1)}, bf16[32,256]{1,0:T(8,128)(2,1)S(1)}, u32[]{:S(2)}, u32[]{:S(2)}) collective-permute-start(bf16[32,256]{1,0:T(8,128)(2,1)S(1)} %constant_dynamic-slice_fusion.refs_8_), channel_id=1, source_target_pairs={{0,24},{1,25},{2,26},{3,27},{4,28},{5,29},{6,30},{7,31},{8,16},{9,... | collective-permute-start | bytes 49160 | tf_op jit(solution)/shard_map/ppermute | solution.py:553
  5.7 1.9 %collective-permute-start.4 = (bf16[64,256]{1,0:T(8,128)(2,1)S(1)}, bf16[64,256]{1,0:T(8,128)(2,1)S(1)}, u32[]{:S(2)}, u32[]{:S(2)}) collective-permute-start(bf16[64,256]{1,0:T(8,128)(2,1)S(1)} %pad_maximum_fusion.2), channel_id=1, source_target_pairs={{0,20},{1,21},{2,22},{3,23},{4,16},{5,17},{6,18},{7,19},{8,28},{9,... | collective-permute-start | bytes 98312 | tf_op jit(solution)/shard_map/ppermute | solution.py:553
  7.6 1.6 %collective-permute-done.4 = bf16[64,256]{1,0:T(8,128)(2,1)S(1)} collective-permute-done((bf16[64,256]{1,0:T(8,128)(2,1)S(1)}, bf16[64,256]{1,0:T(8,128)(2,1)S(1)}, u32[]{:S(2)}, u32[]{:S(2)}) %collective-permute-start.4) | collective-permute-done | bytes 32800 | tf_op jit(solution)/shard_map/ppermute | solution.py:553
  9.2 1.7 %collective-permute-start.5 = (bf16[128,256]{1,0:T(8,128)(2,1)S(1)}, bf16[128,256]{1,0:T(8,128)(2,1)S(1)}, u32[]{:S(2)}, u32[]{:S(2)}) collective-permute-start(bf16[128,256]{1,0:T(8,128)(2,1)S(1)} %pad_maximum_fusion.1), channel_id=1, source_target_pairs={{0,18},{1,19},{2,16},{3,17},{4,22},{5,23},{6,20},{7,21},{8,26},{9,... | collective-permute-start | bytes 196616 | tf_op jit(solution)/shard_map/ppermute | solution.py:553
  11.0 1.6 %copy-done.1 = bf16[1024,8,128]{2,1,0:T(8,128)(2,1)S(1)} copy-done((bf16[1024,8,128]{2,1,0:T(8,128)(2,1)S(1)}, bf16[1024,8,128]{2,1,0:T(8,128)(2,1)}, u32[]{:S(2)}) %copy-start.1) | copy-done | bytes 2097176
  12.5 2.2 %shard_map.28 = (bf16[1024,1024]{1,0:T(8,128)(2,1)S(1)}, bf16[16,1024]{1,0:T(8,128)(2,1)S(1)}, bf16[1024,128]{1,0:T(8,128)(2,1)S(1)}, f32[8,128]{1,0:T(8,128)S(1)}) custom-call(bf16[8192,128]{1,0:T(8,128)(2,1)S(1)} %bitcast.2), custom_call_target="tpu_custom_call" | custom-call | flops 16777216 | tf_op jit(solution)/shard_map/pallas_call | solution.py:46
  16.9 3.9 %collective-permute-done.6.refs_5_ = bf16[256,256]{1,0:T(8,128)(2,1)S(1)} collective-permute-done((bf16[256,256]{1,0:T(8,128)(2,1)S(1)}, bf16[256,256]{1,0:T(8,128)(2,1)S(1)}, u32[]{:S(2)}, u32[]{:S(2)}) %collective-permute-start.6) | collective-permute-done | bytes 131104 | tf_op jit(solution)/shard_map/ppermute | solution.py:553
  22.3 4.5 %collective-permute-start.1 = (bf16[16,1024]{1,0:T(8,128)(2,1)S(1)}, bf16[16,1024]{1,0:T(8,128)(2,1)S(1)}, u32[]{:S(2)}, u32[]{:S(2)}) collective-permute-start(bf16[16,1024]{1,0:T(8,128)(2,1)S(1)} %get-tuple-element.88), channel_id=1, source_target_pairs={{0,1},{1,2},{2,3},{3,4},{4,5},{5,6},{6,7},{7,8},{8,9},{9,10},{10,1... | collective-permute-start | bytes 98312 | tf_op jit(solution)/shard_map/ppermute | solution.py:577
  26.9 1.6 %collective-permute-done.1.refs_2_ = bf16[16,1024]{1,0:T(8,128)(2,1)S(1)} collective-permute-done((bf16[16,1024]{1,0:T(8,128)(2,1)S(1)}, bf16[16,1024]{1,0:T(8,128)(2,1)S(1)}, u32[]{:S(2)}, u32[]{:S(2)}) %collective-permute-start.1) | collective-permute-done | bytes 32800 | tf_op jit(solution)/shard_map/ppermute | solution.py:577
  28.4 6.8 %shard_map.29 = (f32[256,1024]{1,0:T(8,128)S(1)}, bf16[256,256]{1,0:T(8,128)(2,1)S(1)}, bf16[256,256]{1,0:T(8,128)(2,1)S(1)}, f32[256,1024]{1,0:T(8,128)S(1)}, f...) custom-call(bf16[1024,1024]{1,0:T(8,128)(2,1)S(1)} %get-tuple-elemen, ...), custom_call_target="tpu_custom_call" | custom-call | flops 1073741824 | tf_op jit(solution)/shard_map/pallas_call | solution.py:46
  36.5 4.6 %collective-permute-start.10 = (f32[16,128]{1,0:T(8,128)S(1)}, f32[16,128]{1,0:T(8,128)S(1)}, u32[]{:S(2)}, u32[]{:S(2)}) collective-permute-start(f32[16,128]{1,0:T(8,128)S(1)} %get-tuple-element.120), channel_id=1, source_target_pairs={{0,24},{1,25},{2,26},{3,27},{4,28},{5,29},{6,30},{7,31},{8,16},{9,... | collective-permute-start | bytes 24584 | tf_op jit(solution)/shard_map/ppermute | solution.py:553
  42.5 2.8 %collective-permute-start.11 = (f32[16,128]{1,0:T(8,128)S(1)}, f32[16,128]{1,0:T(8,128)S(1)}, u32[]{:S(2)}, u32[]{:S(2)}) collective-permute-start(f32[16,128]{1,0:T(8,128)S(1)} %add.49), channel_id=1, source_target_pairs={{0,20},{1,21},{2,22},{3,23},{4,16},{5,17},{6,18},{7,19},{8,28},{9,... | collective-permute-start | bytes 24584 | tf_op jit(solution)/shard_map/ppermute | solution.py:553
  47.5 3.0 %shard_map.32 = (f32[256,1024]{1,0:T(8,128)S(1)}, f32[256,1024]{1,0:T(8,128)S(1)}, f32[256,1024]{1,0:T(8,128)S(1)}, f32[256,1024]{1,0:T(8,128)S(1)}, f32[40,128]...) custom-call(bf16[256,256]{1,0:T(8,128)(2,1)S(1)} %get-tuple-element.89.refs_0_, ...), custom_call_target="tpu_custom_call" | custom-call | flops 268435456 | tf_op jit(solution)/shard_map/pallas_call | solution.py:46
  51.8 3.1 %collective-permute-done.13.refs_5_ = f32[48,128]{1,0:T(8,128)S(1)} collective-permute-done((f32[48,128]{1,0:T(8,128)S(1)}, f32[48,128]{1,0:T(8,128)S(1)}, u32[]{:S(2)}, u32[]{:S(2)}) %collective-permute-start.13) | collective-permute-done | bytes 24608 | tf_op jit(solution)/shard_map/ppermute | solution.py:553
  56.1 2.4 %shard_map.33 = (f32[256,1024]{1,0:T(8,128)S(1)}, f32[256,1024]{1,0:T(8,128)S(1)}, f32[256,1024]{1,0:T(8,128)S(1)}, f32[256,1024]{1,0:T(8,128)S(1)}, f32[256,128...) custom-call(f32[256,1024]{1,0:T(8,128)S(1)} %get-tuple-element.115.r, ...), custom_call_target="tpu_custom_call" | custom-call | flops 134217728 | tf_op jit(solution)/shard_map/pallas_call | solution.py:46
  58.5 4.0 %collective-permute-start.17 = (f32[16,128]{1,0:T(8,128)S(1)}, f32[16,128]{1,0:T(8,128)S(1)}, u32[]{:S(2)}, u32[]{:S(2)}) collective-permute-start(f32[16,128]{1,0:T(8,128)S(1)} %get-tuple-element.146), channel_id=1, source_target_pairs={{0,24},{1,25},{2,26},{3,27},{4,28},{5,29},{6,30},{7,31},{8,16},{9,... | collective-permute-start | bytes 24584 | tf_op jit(solution)/shard_map/ppermute | solution.py:553
  63.9 2.7 %collective-permute-start.18 = (f32[16,128]{1,0:T(8,128)S(1)}, f32[16,128]{1,0:T(8,128)S(1)}, u32[]{:S(2)}, u32[]{:S(2)}) collective-permute-start(f32[16,128]{1,0:T(8,128)S(1)} %add.54), channel_id=1, source_target_pairs={{0,20},{1,21},{2,22},{3,23},{4,16},{5,17},{6,18},{7,19},{8,28},{9,... | collective-permute-start | bytes 24584 | tf_op jit(solution)/shard_map/ppermute | solution.py:553
  68.2 3.0 %shard_map.35 = (f32[256,1024]{1,0:T(8,128)S(1)}, f32[256,1024]{1,0:T(8,128)S(1)}, f32[256,1024]{1,0:T(8,128)S(1)}, f32[256,1024]{1,0:T(8,128)S(1)}, f32[40,128]...) custom-call(bf16[256,256]{1,0:T(8,128)(2,1)S(1)} %get-tuple-element.89.refs_0_, ...), custom_call_target="tpu_custom_call" | custom-call | flops 268435456 | tf_op jit(solution)/shard_map/pallas_call | solution.py:46
  71.4 2.9 %collective-permute-start.20 = (f32[48,128]{1,0:T(8,128)S(1)}, f32[48,128]{1,0:T(8,128)S(1)}, u32[]{:S(2)}, u32[]{:S(2)}) collective-permute-start(f32[48,128]{1,0:T(8,128)S(1)} %pad_maximum_fusion.4), channel_id=1, source_target_pairs={{0,1},{1,0},{2,3},{3,2},{4,5},{5,4},{6,7},{7,6},{8,9},{9,8},{10,11... | collective-permute-start | bytes 73736 | tf_op jit(solution)/shard_map/ppermute | solution.py:553
  77.3 2.4 %shard_map.36 = (f32[256,1024]{1,0:T(8,128)S(1)}, f32[256,1024]{1,0:T(8,128)S(1)}, f32[256,1024]{1,0:T(8,128)S(1)}, f32[256,1024]{1,0:T(8,128)S(1)}, f32[256,128...) custom-call(f32[256,1024]{1,0:T(8,128)S(1)} %get-tuple-element.141.r, ...), custom_call_target="tpu_custom_call" | custom-call | flops 134217728 | tf_op jit(solution)/shard_map/pallas_call | solution.py:46
  79.7 5.5 %collective-permute-start.23 = (f32[16,128]{1,0:T(8,128)S(1)}, f32[16,128]{1,0:T(8,128)S(1)}, u32[]{:S(2)}, u32[]{:S(2)}) collective-permute-start(f32[16,128]{1,0:T(8,128)S(1)} %get-tuple-element.166), channel_id=1, source_target_pairs={{0,24},{1,25},{2,26},{3,27},{4,28},{5,29},{6,30},{7,31},{8,16},{9,... | collective-permute-start | bytes 24584 | tf_op jit(solution)/shard_map/ppermute | solution.py:553
  86.5 1.7 %collective-permute-start.24 = (f32[16,128]{1,0:T(8,128)S(1)}, f32[16,128]{1,0:T(8,128)S(1)}, u32[]{:S(2)}, u32[]{:S(2)}) collective-permute-start(f32[16,128]{1,0:T(8,128)S(1)} %add.59), channel_id=1, source_target_pairs={{0,20},{1,21},{2,22},{3,23},{4,16},{5,17},{6,18},{7,19},{8,28},{9,... | collective-permute-start | bytes 24584 | tf_op jit(solution)/shard_map/ppermute | solution.py:553
  90.4 2.3 %collective-permute-done.25 = f32[16,128]{1,0:T(8,128)S(1)} collective-permute-done((f32[16,128]{1,0:T(8,128)S(1)}, f32[16,128]{1,0:T(8,128)S(1)}, u32[]{:S(2)}, u32[]{:S(2)}) %collective-permute-start.25) | collective-permute-done | bytes 8224 | tf_op jit(solution)/shard_map/ppermute | solution.py:553
  95.8 1.9 %collective-permute-start.27 = (f32[16,128]{1,0:T(8,128)S(1)}, f32[16,128]{1,0:T(8,128)S(1)}, u32[]{:S(2)}, u32[]{:S(2)}) collective-permute-start(f32[16,128]{1,0:T(8,128)S(1)} %add.62), channel_id=1, source_target_pairs={{0,16},{1,17},{2,18},{3,19},{4,20},{5,21},{6,22},{7,23},{8,24},{9,... | collective-permute-start | bytes 24584 | tf_op jit(solution)/shard_map/ppermute | solution.py:553
  (69 shorter events, 28.4 us)
Async XLA Ops:
  0.8 4.9 %collective-permute-start.3 = (bf16[32,256]{1,0:T(8,128)(2,1)S(1)}, bf16[32,256]{1,0:T(8,128)(2,1)S(1)}, u32[]{:S(2)}, u32[]{:S(2)}) collective-permute-start(bf16[32,256]{1,0:T(8,128)(2,1)S(1)} %constant_dynamic-slice_fusion.refs_8_), channel_id=1, source_target_pairs={{0,24},{1,25},{2,26},{3,27},{4,28},{5,29},{6,30},{7,31},{8,16},{9,... | collective-permute-start | bytes 49160 | tf_op jit(solution)/shard_map/ppermute | solution.py:553
  5.7 3.5 %collective-permute-start.4 = (bf16[64,256]{1,0:T(8,128)(2,1)S(1)}, bf16[64,256]{1,0:T(8,128)(2,1)S(1)}, u32[]{:S(2)}, u32[]{:S(2)}) collective-permute-start(bf16[64,256]{1,0:T(8,128)(2,1)S(1)} %pad_maximum_fusion.2), channel_id=1, source_target_pairs={{0,20},{1,21},{2,22},{3,23},{4,16},{5,17},{6,18},{7,19},{8,28},{9,... | collective-permute-start | bytes 98312 | tf_op jit(solution)/shard_map/ppermute | solution.py:553
  9.2 6.0 %collective-permute-start.5 = (bf16[128,256]{1,0:T(8,128)(2,1)S(1)}, bf16[128,256]{1,0:T(8,128)(2,1)S(1)}, u32[]{:S(2)}, u32[]{:S(2)}) collective-permute-start(bf16[128,256]{1,0:T(8,128)(2,1)S(1)} %pad_maximum_fusion.1), channel_id=1, source_target_pairs={{0,18},{1,19},{2,16},{3,17},{4,22},{5,23},{6,20},{7,21},{8,26},{9,... | collective-permute-start | bytes 196616 | tf_op jit(solution)/shard_map/ppermute | solution.py:553
  14.7 13.7 %collective-permute-start = (bf16[1024,128]{1,0:T(8,128)(2,1)S(1)}, bf16[1024,128]{1,0:T(8,128)(2,1)S(1)}, u32[]{:S(2)}, u32[]{:S(2)}) collective-permute-start(bf16[1024,128]{1,0:T(8,128)(2,1)S(1)} %get-tuple-element.87), channel_id=1, source_target_pairs={{0,16},{1,17},{2,18},{3,19},{4,20},{5,21},{6,22},{7,23},{8,24},{9,... | collective-permute-start | bytes 786440 | tf_op jit(solution)/shard_map/ppermute | solution.py:553
  15.3 5.6 %collective-permute-start.6 = (bf16[256,256]{1,0:T(8,128)(2,1)S(1)}, bf16[256,256]{1,0:T(8,128)(2,1)S(1)}, u32[]{:S(2)}, u32[]{:S(2)}) collective-permute-start(bf16[256,256]{1,0:T(8,128)(2,1)S(1)} %pad_maximum_fusion.refs_4_), channel_id=1, source_target_pairs={{0,17},{1,16},{2,19},{3,18},{4,21},{5,20},{6,23},{7,22},{8,25},{9,... | collective-permute-start | bytes 393224 | tf_op jit(solution)/shard_map/ppermute | solution.py:553
  16.5 11.9 %collective-permute-start.7 = (bf16[256,256]{1,0:T(8,128)(2,1)S(1)}, bf16[256,256]{1,0:T(8,128)(2,1)S(1)}, u32[]{:S(2)}, u32[]{:S(2)}) collective-permute-start(bf16[256,256]{1,0:T(8,128)(2,1)S(1)} %pad_maximum_fusion.refs_4_), channel_id=1, source_target_pairs={{0,16},{1,17},{2,18},{3,19},{4,20},{5,21},{6,22},{7,23},{8,24},{9,... | collective-permute-start | bytes 393224 | tf_op jit(solution)/shard_map/ppermute | solution.py:553
  20.9 7.5 %collective-permute-start.8 = (bf16[256,256]{1,0:T(8,128)(2,1)S(1)}, bf16[256,256]{1,0:T(8,128)(2,1)S(1)}, u32[]{:S(2)}, u32[]{:S(2)}) collective-permute-start(bf16[256,256]{1,0:T(8,128)(2,1)S(1)} %collective-permute-done.6.refs_5_), channel_id=1, source_target_pairs={{0,16},{1,17},{2,18},{3,19},{4,20},{5,21},{6,22},{7,23},{8,24},{9,... | collective-permute-start | bytes 393224 | tf_op jit(solution)/shard_map/ppermute | solution.py:553
  21.0 5.8 %collective-permute-start.2 = (bf16[16,1024]{1,0:T(8,128)(2,1)S(1)}, bf16[16,1024]{1,0:T(8,128)(2,1)S(1)}, u32[]{:S(2)}, u32[]{:S(2)}) collective-permute-start(bf16[16,1024]{1,0:T(8,128)(2,1)S(1)} %get-tuple-element.88), channel_id=1, source_target_pairs={{1,0},{2,1},{3,2},{4,3},{5,4},{6,5},{7,6},{8,7},{9,8},{10,9},{11,1... | collective-permute-start | bytes 98312 | tf_op jit(solution)/shard_map/ppermute | solution.py:577
  22.3 6.1 %collective-permute-start.1 = (bf16[16,1024]{1,0:T(8,128)(2,1)S(1)}, bf16[16,1024]{1,0:T(8,128)(2,1)S(1)}, u32[]{:S(2)}, u32[]{:S(2)}) collective-permute-start(bf16[16,1024]{1,0:T(8,128)(2,1)S(1)} %get-tuple-element.88), channel_id=1, source_target_pairs={{0,1},{1,2},{2,3},{3,4},{4,5},{5,6},{6,7},{7,8},{8,9},{9,10},{10,1... | collective-permute-start | bytes 98312 | tf_op jit(solution)/shard_map/ppermute | solution.py:577
  36.5 6.0 %collective-permute-start.10 = (f32[16,128]{1,0:T(8,128)S(1)}, f32[16,128]{1,0:T(8,128)S(1)}, u32[]{:S(2)}, u32[]{:S(2)}) collective-permute-start(f32[16,128]{1,0:T(8,128)S(1)} %get-tuple-element.120), channel_id=1, source_target_pairs={{0,24},{1,25},{2,26},{3,27},{4,28},{5,29},{6,30},{7,31},{8,16},{9,... | collective-permute-start | bytes 24584 | tf_op jit(solution)/shard_map/ppermute | solution.py:553
  42.5 4.2 %collective-permute-start.11 = (f32[16,128]{1,0:T(8,128)S(1)}, f32[16,128]{1,0:T(8,128)S(1)}, u32[]{:S(2)}, u32[]{:S(2)}) collective-permute-start(f32[16,128]{1,0:T(8,128)S(1)} %add.49), channel_id=1, source_target_pairs={{0,20},{1,21},{2,22},{3,23},{4,16},{5,17},{6,18},{7,19},{8,28},{9,... | collective-permute-start | bytes 24584 | tf_op jit(solution)/shard_map/ppermute | solution.py:553
  46.8 4.3 %collective-permute-start.12 = (f32[16,128]{1,0:T(8,128)S(1)}, f32[16,128]{1,0:T(8,128)S(1)}, u32[]{:S(2)}, u32[]{:S(2)}) collective-permute-start(f32[16,128]{1,0:T(8,128)S(1)} %add.50), channel_id=1, source_target_pairs={{0,18},{1,19},{2,16},{3,17},{4,22},{5,23},{6,20},{7,21},{8,26},{9,... | collective-permute-start | bytes 24584 | tf_op jit(solution)/shard_map/ppermute | solution.py:553
  50.5 5.6 %collective-permute-start.9 = (f32[512,128]{1,0:T(8,128)S(1)}, f32[512,128]{1,0:T(8,128)S(1)}, u32[]{:S(2)}, u32[]{:S(2)}) collective-permute-start(f32[512,128]{1,0:T(8,128)S(1)} %get-tuple-element.119), channel_id=1, source_target_pairs={{0,16},{1,17},{2,18},{3,19},{4,20},{5,21},{6,22},{7,23},{8,24},{9,... | collective-permute-start | bytes 786440 | tf_op jit(solution)/shard_map/ppermute | solution.py:553
  51.0 3.9 %collective-permute-start.13 = (f32[48,128]{1,0:T(8,128)S(1)}, f32[48,128]{1,0:T(8,128)S(1)}, u32[]{:S(2)}, u32[]{:S(2)}) collective-permute-start(f32[48,128]{1,0:T(8,128)S(1)} %pad_maximum_fusion.3), channel_id=1, source_target_pairs={{0,1},{1,0},{2,3},{3,2},{4,5},{5,4},{6,7},{7,6},{8,9},{9,8},{10,11... | collective-permute-start | bytes 73736 | tf_op jit(solution)/shard_map/ppermute | solution.py:553
  51.1 5.0 %collective-permute-start.14 = (f32[32,128]{1,0:T(8,128)S(1)}, f32[32,128]{1,0:T(8,128)S(1)}, u32[]{:S(2)}, u32[]{:S(2)}) collective-permute-start(f32[32,128]{1,0:T(8,128)S(1)} %get-tuple-element.122), channel_id=1, source_target_pairs={{1,2},{2,1},{3,4},{4,3},{5,6},{6,5},{7,8},{8,7},{9,10},{10,9},{11,... | collective-permute-start | bytes 49160 | tf_op jit(solution)/shard_map/ppermute | solution.py:592
  58.5 5.3 %collective-permute-start.17 = (f32[16,128]{1,0:T(8,128)S(1)}, f32[16,128]{1,0:T(8,128)S(1)}, u32[]{:S(2)}, u32[]{:S(2)}) collective-permute-start(f32[16,128]{1,0:T(8,128)S(1)} %get-tuple-element.146), channel_id=1, source_target_pairs={{0,24},{1,25},{2,26},{3,27},{4,28},{5,29},{6,30},{7,31},{8,16},{9,... | collective-permute-start | bytes 24584 | tf_op jit(solution)/shard_map/ppermute | solution.py:553
  63.9 4.2 %collective-permute-start.18 = (f32[16,128]{1,0:T(8,128)S(1)}, f32[16,128]{1,0:T(8,128)S(1)}, u32[]{:S(2)}, u32[]{:S(2)}) collective-permute-start(f32[16,128]{1,0:T(8,128)S(1)} %add.54), channel_id=1, source_target_pairs={{0,20},{1,21},{2,22},{3,23},{4,16},{5,17},{6,18},{7,19},{8,28},{9,... | collective-permute-start | bytes 24584 | tf_op jit(solution)/shard_map/ppermute | solution.py:553
  68.1 3.2 %collective-permute-start.19 = (f32[16,128]{1,0:T(8,128)S(1)}, f32[16,128]{1,0:T(8,128)S(1)}, u32[]{:S(2)}, u32[]{:S(2)}) collective-permute-start(f32[16,128]{1,0:T(8,128)S(1)} %add.55), channel_id=1, source_target_pairs={{0,18},{1,19},{2,16},{3,17},{4,22},{5,23},{6,20},{7,21},{8,26},{9,... | collective-permute-start | bytes 24584 | tf_op jit(solution)/shard_map/ppermute | solution.py:553
  71.2 6.1 %collective-permute-start.16 = (f32[512,128]{1,0:T(8,128)S(1)}, f32[512,128]{1,0:T(8,128)S(1)}, u32[]{:S(2)}, u32[]{:S(2)}) collective-permute-start(f32[512,128]{1,0:T(8,128)S(1)} %get-tuple-element.145), channel_id=1, source_target_pairs={{0,16},{1,17},{2,18},{3,19},{4,20},{5,21},{6,22},{7,23},{8,24},{9,... | collective-permute-start | bytes 786440 | tf_op jit(solution)/shard_map/ppermute | solution.py:553
  71.4 4.7 %collective-permute-start.20 = (f32[48,128]{1,0:T(8,128)S(1)}, f32[48,128]{1,0:T(8,128)S(1)}, u32[]{:S(2)}, u32[]{:S(2)}) collective-permute-start(f32[48,128]{1,0:T(8,128)S(1)} %pad_maximum_fusion.4), channel_id=1, source_target_pairs={{0,1},{1,0},{2,3},{3,2},{4,5},{5,4},{6,7},{7,6},{8,9},{9,8},{10,11... | collective-permute-start | bytes 73736 | tf_op jit(solution)/shard_map/ppermute | solution.py:553
  79.7 6.8 %collective-permute-start.23 = (f32[16,128]{1,0:T(8,128)S(1)}, f32[16,128]{1,0:T(8,128)S(1)}, u32[]{:S(2)}, u32[]{:S(2)}) collective-permute-start(f32[16,128]{1,0:T(8,128)S(1)} %get-tuple-element.166), channel_id=1, source_target_pairs={{0,24},{1,25},{2,26},{3,27},{4,28},{5,29},{6,30},{7,31},{8,16},{9,... | collective-permute-start | bytes 24584 | tf_op jit(solution)/shard_map/ppermute | solution.py:553
  86.5 3.1 %collective-permute-start.24 = (f32[16,128]{1,0:T(8,128)S(1)}, f32[16,128]{1,0:T(8,128)S(1)}, u32[]{:S(2)}, u32[]{:S(2)}) collective-permute-start(f32[16,128]{1,0:T(8,128)S(1)} %add.59), channel_id=1, source_target_pairs={{0,20},{1,21},{2,22},{3,23},{4,16},{5,17},{6,18},{7,19},{8,28},{9,... | collective-permute-start | bytes 24584 | tf_op jit(solution)/shard_map/ppermute | solution.py:553
  89.6 3.1 %collective-permute-start.25 = (f32[16,128]{1,0:T(8,128)S(1)}, f32[16,128]{1,0:T(8,128)S(1)}, u32[]{:S(2)}, u32[]{:S(2)}) collective-permute-start(f32[16,128]{1,0:T(8,128)S(1)} %add.60), channel_id=1, source_target_pairs={{0,18},{1,19},{2,16},{3,17},{4,22},{5,23},{6,20},{7,21},{8,26},{9,... | collective-permute-start | bytes 24584 | tf_op jit(solution)/shard_map/ppermute | solution.py:553
  92.7 3.1 %collective-permute-start.26 = (f32[16,128]{1,0:T(8,128)S(1)}, f32[16,128]{1,0:T(8,128)S(1)}, u32[]{:S(2)}, u32[]{:S(2)}) collective-permute-start(f32[16,128]{1,0:T(8,128)S(1)} %add.61), channel_id=1, source_target_pairs={{0,17},{1,16},{2,19},{3,18},{4,21},{5,20},{6,23},{7,22},{8,25},{9,... | collective-permute-start | bytes 24584 | tf_op jit(solution)/shard_map/ppermute | solution.py:553
  (6 other events, 10.6 us)

commit v2 on v1

--- a/solution.py
+++ b/solution.py
@@ -42,11 +42,11 @@
     return jnp.minimum(jnp.maximum(value, -bound), bound)
 
 
-def call(body, outs, args, scratch=(), flops=0, limit=24):
+def call(body, outs, args, scratch=(), flops=0, limit=24, space=pltpu.VMEM):
     return pl.pallas_call(
         body,
         out_shape=[jax.ShapeDtypeStruct(*out) for out in outs],
-        in_specs=[pl.BlockSpec(memory_space=pltpu.VMEM)] * len(args),
+        in_specs=[pl.BlockSpec(memory_space=space)] * len(args),
         out_specs=[pl.BlockSpec(memory_space=pltpu.VMEM)] * len(outs),
         scratch_shapes=list(scratch),
         cost_estimate=pl.CostEstimate(flops=flops, bytes_accessed=0, transcendentals=0),
@@ -124,22 +124,33 @@
         store(start, block, dot(inv_high[...], high) + (dot(inv_high[...], low) + dot(inv_low[...], high)))
 
 
-def survey_kernel(rows, cols, observed, flat, columns, row_edge, norm, wide_band):
+def survey_kernel(rows, cols, observed, flat, columns, row_edge, norm, band, wide_band, arrived):
     channels, pixels = flat.shape
     tall = 2 * GROUP
     zero = jnp.zeros((tall, cols), F32)
+    parts = arrived.shape[0]
+    size = channels * rows // parts
+    copies = []
+    for part in range(parts):
+        here = pl.ds(part * size, size)
+        copies.append(pltpu.make_async_copy(observed.at[here, :], band.at[here, :], arrived.at[part]))
+        copies[-1].start()
 
     def widen(index, total):
         total = list(total)
         for part in range(rows):
             here = pl.ds(pl.multiple_of((index * rows + part) * tall, tall), tall)
-            value = observed[here, :].astype(F32)
+            value = band[here, :].astype(F32)
             wide_band[here, :] = value
             total[part % 2] = total[part % 2] + value * value
         return tuple(total)
 
-    even, odd = lax.fori_loop(0, channels // tall, widen, (zero, zero), unroll=4)
-    total = even + odd
+    total = (zero, zero)
+    steps = channels // tall // parts
+    for part in range(parts):
+        copies[part].wait()
+        total = lax.fori_loop(part * steps, (part + 1) * steps, widen, total, unroll=4)
+    total = total[0] + total[1]
     norm[...] = total[:GROUP, :] + total[GROUP:, :]
 
     def place(index, carry):
@@ -168,27 +179,73 @@
         row_edge[...] = flat[:, :cols]
 
 
+def gather_half(observed, first_half, second_half, order, half, library_part, band_part):
+    blocks = len(order)
+    rows = first_half.shape[0] // blocks
+    own = lax.axis_index("col")
+    for block in range(blocks):
+        at = block * 2 * rows
+        source = slice(block * rows, (block + 1) * rows)
+        library_part[pl.ds(pl.multiple_of(at + half * rows, rows), rows), :] = first_half[source, :]
+        library_part[pl.ds(pl.multiple_of(at + (1 - half) * rows, rows), rows), :] = second_half[source, :]
+        base = pl.multiple_of((own ^ order[block]) * (2 * rows), 2 * rows)
+        band_part[at : at + 2 * rows, :] = observed[pl.ds(base, 2 * rows), :]
+
+
+def own_half():
+    parity = lax.axis_index("row")
+    bits = lax.axis_index("col")
+    for _ in range(max(1, (lax.axis_size("col") - 1).bit_length())):
+        parity = parity ^ (bits & 1)
+        bits = bits >> 1
+    return parity
+
+
+def early_kernel(order, observed, mine, other, projected, gram, library_part, band_part):
+    gather_half(observed, mine, other, order, own_half(), library_part, band_part)
+    pixels = band_part.shape[1]
+    for start in range(0, pixels, 512):
+        span = slice(start, min(start + 512, pixels))
+        projected[:, span] = dot_columns(library_part[...], band_part[:, span])
+    gram[...] = dot_columns(library_part[...], library_part[...])
+
+
 def start_kernel(rows, cols, order, *refs):
     ordered = order is True
-    observed, row_halo, left_halo, right_halo = refs[:4]
-    inputs = 5 if ordered else 9
+    observed, row_halo, from_pair, from_next = refs[:4]
+    inputs = 5 if ordered else 11
     pieces = refs[4:inputs]
     projected, inv_high, inv_low, fit, fit_gram, quad, near_row, near_left, near_right = refs[inputs : inputs + 9]
     inverse, power, rhs_high, rhs_low, left, panel = refs[inputs + 9 : inputs + 15]
     if ordered:
         full = pieces[0]
     else:
-        full = refs[inputs + 15]
-        place_library(pieces, full, order)
+        full, library_part, band_part = refs[inputs + 15 :]
+        place_library(pieces[:5], full, order)
+        early, early_gram = pieces[5:]
+        late = order[len(order) // 2 :]
+        gather_half(observed, pieces[1], pieces[3], late, own_half(), library_part, band_part)
     members = full.shape[1]
     pixels = rows * cols
     panel[...] = jnp.zeros(panel.shape, BF16)
-    panel[0 : 2 * rows, :] = right_halo[...]
-    panel[2 * rows : 4 * rows, :] = left_halo[...]
+    is_odd = (lax.axis_index("col") & 1) > 0
+    for low, odd_one, even_one in ((0, from_next, from_pair), (2 * rows, from_pair, from_next)):
+
+        @pl.when(is_odd)
+        def _():
+            panel[low : low + 2 * rows, :] = odd_one[...]
+
+        @pl.when(jnp.logical_not(is_odd))
+        def _():
+            panel[low : low + 2 * rows, :] = even_one[...]
+
     block = min(512, pixels)
     for start in range(0, pixels, block):
         span = slice(start, start + block)
-        result = dot_columns(full[...], observed[:, span])
+        if ordered:
+            result = dot_columns(full[...], observed[:, span])
+        else:
+            result = early[:, span] + dot_columns(library_part[...], band_part[:, span])
         projected[:, span] = result
         rhs_high[:, span], rhs_low[:, span] = split(result)
     span = slice(pixels, pixels + cols)
@@ -196,7 +253,11 @@
     span = slice(pixels + cols, pixels + cols + panel.shape[0])
     beside = lax.dot_general(full[...], panel[...], (((0,), (1,)), ((), ())), preferred_element_type=F32)
     rhs_high[:, span], rhs_low[:, span] = split(beside)
-    invert(dot_columns(full[...], full[...]), inverse, power, left)
+    if ordered:
+        gram = dot_columns(full[...], full[...])
+    else:
+        gram = early_gram[...] + dot_columns(library_part[...], library_part[...])
+    invert(gram, inverse, power, left)
     inv_high[...], inv_low[...] = split(inverse[...])
 
     def store(start, size, value):
@@ -571,17 +632,16 @@
     return value
 
 
-def shifted(value, axis, step):
-    count = lax.axis_size(axis)
-    first, last = max(0, -step), min(count, count - step)
-    return lax.ppermute(value, axis, [(source, source + step) for source in range(first, last)])
-
-
 def band_halos(row_edge, columns):
+    from_next = next_swap(columns)
+    from_pair = pair_swap(columns)
     near_row = flat_swap(row_edge, 0, True)
-    near_left = shifted(columns, "col", 1)
-    near_right = shifted(columns, "col", -1)
-    return near_row, near_left, near_right
+    return near_row, from_pair, from_next
+
+
+def pair_swap(value):
+    count = lax.axis_size("col")
+    return lax.ppermute(value, "col", [(c, c ^ 1) for c in range(count) if c ^ 1 < count])
 
 
 def next_swap(value):
@@ -597,9 +657,8 @@
     near_row = flat_swap(row_edge, 0, True)
     from_next = next_swap(to_next)
     if not regular():
-        both = jnp.concatenate([value, to_pair], axis=0)
-        pairs = [(c, c ^ 1) for c in range(lax.axis_size("col")) if c ^ 1 < lax.axis_size("col")]
-        return lax.psum(value, ("row", "col")), near_row, lax.ppermute(both, "col", pairs), from_next
+        from_pair = pair_swap(jnp.concatenate([value, to_pair], axis=0))
+        return lax.psum(value, ("row", "col")), near_row, from_pair, from_next
     stages = strides()
     for stride in stages[:-1]:
         value = value + flat_swap(value, stride, True)
@@ -645,7 +704,13 @@
         functools.partial(survey_kernel, rows, cols),
         [((channels, pixels), BF16), ((2 * rows, channels), BF16), ((channels, cols), BF16), scalar],
         [observed.reshape(channels * rows, cols)],
-        [pltpu.VMEM((channels * rows, cols), F32)],
+        [
+            pltpu.VMEM((channels * rows, cols), BF16),
+            pltpu.VMEM((channels * rows, cols), F32),
+            pltpu.SemaphoreType.DMA((4,)),
+        ],
+        space=pltpu.HBM,
+        limit=50,
         flops=2 * rows * channels * pixels,
     )
     near = band_halos(row_edge, columns)
@@ -659,9 +724,17 @@
         pltpu.SMEM((2,), F32),
         pltpu.VMEM((cols, channels), BF16),
     ]
+    work = 2 * members * members * pixels
     if order is not True:
-        scratch.append(pltpu.VMEM((channels, members), BF16))
-    work = 2 * members * members * pixels
+        parts = [pltpu.VMEM((channels // 2, members), BF16), pltpu.VMEM((channels // 2, pixels), BF16)]
+        scratch += [pltpu.VMEM((channels, members), BF16), *parts]
+        pieces += call(
+            functools.partial(early_kernel, order[: len(order) // 2]),
+            [field, ((members, members), F32)],
+            [flat, pieces[0], pieces[2]],
+            parts,
+            flops=4 * work,
+        )
     projected, inv_high, inv_low, fit, fit_gram, quad, *near = call(
         functools.partial(start_kernel, rows, cols, order),
         [field, half, half, field, field, ((2 * GROUP, cols), F32), strip, strip, strip],

time: 100 us -> 96.2 us (0.962)
  waiting for transfers between devices: 23.6 us -> 21.6 us
  starting transfers between devices: 45.9 us -> 44.3 us
  local copies, waits for them, and re-layouts: 2.35 us -> 0.76 us
  Pallas kernels: 28 us -> 29 us
    ppermute x2 -> x1, starting transfers between devices: 5.83 us -> 3.3 us  [pair_swap(): lax.ppermute(value, 'col', [(c, c ^ 1) for c in range(count) if c ^ 1 < c...]
    ppermute x24, waiting for transfers between devices: 22 us -> 19.9 us  [flat_swap(): return lax.ppermute(value, ('row', 'col'), pairs)]
    unnamed x4 -> x2, local copies, waits for them, and re-layouts: 2.35 us -> 0.76 us
    pallas_call x12 -> x13, Pallas kernels: 28 us -> 29 us  [call(): pl.pallas_call(body, out_shape=[jax.ShapeDtypeStruct(*out) for out in out...]
    ppermute x2 -> x3, starting transfers between devices: 1.49 us -> 2.13 us  [next_swap(): return lax.ppermute(value, 'col', pairs)]
  transfers between devices with their start and end apart: 28 -> 28, of which waited for: 14 -> 13; matrix products, arithmetic and copies ran while one was open for 0% -> 0% of each run, Pallas kernels for 14% -> 16%
where the time goes in v2:
time: 96.2 us; the launch traced here: 96 us
  starting transfers between devices  44.3 us (46%)
  Pallas kernels  29 us (30%)
  waiting for transfers between devices  21.6 us (22%)
    ppermute x24, starting transfers between devices, flat_swap(): return lax.ppermute(value, ('row', 'col'), pairs)  38.9 us
    pallas_call x13, Pallas kernels, call(): pl.pallas_call(body, out_shape=[jax.ShapeDtypeStruct(*out) for out in out...  29 us
    ppermute x24, waiting for transfers between devices, flat_swap(): return lax.ppermute(value, ('row', 'col'), pairs)  19.9 us
    ppermute x1, starting transfers between devices, pair_swap(): lax.ppermute(value, 'col', [(c, c ^ 1) for c in range(count) if c ^ 1 < c...  3.3 us
    ppermute x3, starting transfers between devices, next_swap(): return lax.ppermute(value, 'col', pairs)  2.13 us
  transfers between devices with their start and end apart: 28, of which 13 were waited for; matrix products, arithmetic and copies ran while one was open for 0% of the time, Pallas kernels for 16%

profile of v2, /device:TPU:0, one launch (start us, length us, event | category | flops | bytes accessed | tf_op | source)
XLA Modules:
  0.0 96.0 jit_solution(11465818927065683193)
XLA Ops:
  0.8 3.5 %collective-permute-start.3 = (bf16[32,256]{1,0:T(8,128)(2,1)S(1)}, bf16[32,256]{1,0:T(8,128)(2,1)S(1)}, u32[]{:S(2)}, u32[]{:S(2)}) collective-permute-start(bf16[32,256]{1,0:T(8,128)(2,1)S(1)} %constant_dynamic-slice_fusion.refs_8_), channel_id=1, source_target_pairs={{0,24},{1,25},{2,26},{3,27},{4,28},{5,29},{6,30},{7,31},{8,16},{9,... | collective-permute-start | bytes 49160 | tf_op jit(solution)/shard_map/ppermute | solution.py:614
  5.7 1.9 %collective-permute-start.4 = (bf16[64,256]{1,0:T(8,128)(2,1)S(1)}, bf16[64,256]{1,0:T(8,128)(2,1)S(1)}, u32[]{:S(2)}, u32[]{:S(2)}) collective-permute-start(bf16[64,256]{1,0:T(8,128)(2,1)S(1)} %pad_maximum_fusion.2), channel_id=1, source_target_pairs={{0,20},{1,21},{2,22},{3,23},{4,16},{5,17},{6,18},{7,19},{8,28},{9,... | collective-permute-start | bytes 98312 | tf_op jit(solution)/shard_map/ppermute | solution.py:614
  7.6 1.6 %collective-permute-done.4 = bf16[64,256]{1,0:T(8,128)(2,1)S(1)} collective-permute-done((bf16[64,256]{1,0:T(8,128)(2,1)S(1)}, bf16[64,256]{1,0:T(8,128)(2,1)S(1)}, u32[]{:S(2)}, u32[]{:S(2)}) %collective-permute-start.4) | collective-permute-done | bytes 32800 | tf_op jit(solution)/shard_map/ppermute | solution.py:614
  9.2 1.7 %collective-permute-start.5 = (bf16[128,256]{1,0:T(8,128)(2,1)S(1)}, bf16[128,256]{1,0:T(8,128)(2,1)S(1)}, u32[]{:S(2)}, u32[]{:S(2)}) collective-permute-start(bf16[128,256]{1,0:T(8,128)(2,1)S(1)} %pad_maximum_fusion.1), channel_id=1, source_target_pairs={{0,18},{1,19},{2,16},{3,17},{4,22},{5,23},{6,20},{7,21},{8,26},{9,... | collective-permute-start | bytes 196616 | tf_op jit(solution)/shard_map/ppermute | solution.py:614
  10.9 3.3 %shard_map.28 = (bf16[1024,1024]{1,0:T(8,128)(2,1)S(1)}, bf16[16,1024]{1,0:T(8,128)(2,1)S(1)}, bf16[1024,128]{1,0:T(8,128)(2,1)S(1)}, f32[8,128]{1,0:T(8,128)S(1)}) custom-call(bf16[8192,128]{1,0:T(8,128)(2,1)} %bitcast.2), custom_call_target="tpu_custom_call" | custom-call | flops 16777216 | tf_op jit(solution)/shard_map/pallas_call | solution.py:46
  16.4 3.9 %collective-permute-done.6.refs_5_ = bf16[256,256]{1,0:T(8,128)(2,1)S(1)} collective-permute-done((bf16[256,256]{1,0:T(8,128)(2,1)S(1)}, bf16[256,256]{1,0:T(8,128)(2,1)S(1)}, u32[]{:S(2)}, u32[]{:S(2)}) %collective-permute-start.6) | collective-permute-done | bytes 131104 | tf_op jit(solution)/shard_map/ppermute | solution.py:614
  21.1 3.3 %collective-permute-start.1 = (bf16[16,1024]{1,0:T(8,128)(2,1)S(1)}, bf16[16,1024]{1,0:T(8,128)(2,1)S(1)}, u32[]{:S(2)}, u32[]{:S(2)}) collective-permute-start(bf16[16,1024]{1,0:T(8,128)(2,1)S(1)} %get-tuple-element.90), channel_id=1, source_target_pairs={{0,1},{1,0},{2,3},{3,2},{4,5},{5,4},{6,7},{7,6},{8,9},{9,8},{10,11... | collective-permute-start | bytes 98312 | tf_op jit(solution)/shard_map/ppermute | solution.py:644
  25.0 1.7 %collective-permute-done.1.refs_2_ = bf16[16,1024]{1,0:T(8,128)(2,1)S(1)} collective-permute-done((bf16[16,1024]{1,0:T(8,128)(2,1)S(1)}, bf16[16,1024]{1,0:T(8,128)(2,1)S(1)}, u32[]{:S(2)}, u32[]{:S(2)}) %collective-permute-start.1) | collective-permute-done | bytes 32800 | tf_op jit(solution)/shard_map/ppermute | solution.py:644
  26.7 6.2 %shard_map.30 = (f32[256,1024]{1,0:T(8,128)S(1)}, bf16[256,256]{1,0:T(8,128)(2,1)S(1)}, bf16[256,256]{1,0:T(8,128)(2,1)S(1)}, f32[256,1024]{1,0:T(8,128)S(1)}, f...) custom-call(bf16[1024,1024]{1,0:T(8,128)(2,1)S(1)} %get-tuple-elemen, ...), custom_call_target="tpu_custom_call" | custom-call | flops 1073741824 | tf_op jit(solution)/shard_map/pallas_call | solution.py:46
  34.2 2.9 %collective-permute-start.10 = (f32[16,128]{1,0:T(8,128)S(1)}, f32[16,128]{1,0:T(8,128)S(1)}, u32[]{:S(2)}, u32[]{:S(2)}) collective-permute-start(f32[16,128]{1,0:T(8,128)S(1)} %get-tuple-element.124), channel_id=1, source_target_pairs={{0,24},{1,25},{2,26},{3,27},{4,28},{5,29},{6,30},{7,31},{8,16},{9,... | collective-permute-start | bytes 24584 | tf_op jit(solution)/shard_map/ppermute | solution.py:614
  38.6 2.9 %collective-permute-start.11 = (f32[16,128]{1,0:T(8,128)S(1)}, f32[16,128]{1,0:T(8,128)S(1)}, u32[]{:S(2)}, u32[]{:S(2)}) collective-permute-start(f32[16,128]{1,0:T(8,128)S(1)} %add.49), channel_id=1, source_target_pairs={{0,20},{1,21},{2,22},{3,23},{4,16},{5,17},{6,18},{7,19},{8,28},{9,... | collective-permute-start | bytes 24584 | tf_op jit(solution)/shard_map/ppermute | solution.py:614
  43.7 3.0 %shard_map.33 = (f32[256,1024]{1,0:T(8,128)S(1)}, f32[256,1024]{1,0:T(8,128)S(1)}, f32[256,1024]{1,0:T(8,128)S(1)}, f32[256,1024]{1,0:T(8,128)S(1)}, f32[40,128]...) custom-call(bf16[256,256]{1,0:T(8,128)(2,1)S(1)} %get-tuple-element.93.refs_0_, ...), custom_call_target="tpu_custom_call" | custom-call | flops 268435456 | tf_op jit(solution)/shard_map/pallas_call | solution.py:46
  52.3 2.4 %shard_map.34 = (f32[256,1024]{1,0:T(8,128)S(1)}, f32[256,1024]{1,0:T(8,128)S(1)}, f32[256,1024]{1,0:T(8,128)S(1)}, f32[256,1024]{1,0:T(8,128)S(1)}, f32[256,128...) custom-call(f32[256,1024]{1,0:T(8,128)S(1)} %get-tuple-element.119.r, ...), custom_call_target="tpu_custom_call" | custom-call | flops 134217728 | tf_op jit(solution)/shard_map/pallas_call | solution.py:46
  54.7 5.1 %collective-permute-start.17 = (f32[16,128]{1,0:T(8,128)S(1)}, f32[16,128]{1,0:T(8,128)S(1)}, u32[]{:S(2)}, u32[]{:S(2)}) collective-permute-start(f32[16,128]{1,0:T(8,128)S(1)} %get-tuple-element.150), channel_id=1, source_target_pairs={{0,24},{1,25},{2,26},{3,27},{4,28},{5,29},{6,30},{7,31},{8,16},{9,... | collective-permute-start | bytes 24584 | tf_op jit(solution)/shard_map/ppermute | solution.py:614
  61.2 1.9 %collective-permute-start.18 = (f32[16,128]{1,0:T(8,128)S(1)}, f32[16,128]{1,0:T(8,128)S(1)}, u32[]{:S(2)}, u32[]{:S(2)}) collective-permute-start(f32[16,128]{1,0:T(8,128)S(1)} %add.54), channel_id=1, source_target_pairs={{0,20},{1,21},{2,22},{3,23},{4,16},{5,17},{6,18},{7,19},{8,28},{9,... | collective-permute-start | bytes 24584 | tf_op jit(solution)/shard_map/ppermute | solution.py:614
  63.1 1.6 %shard_map.35 = (bf16[256,2048]{1,0:T(8,128)(2,1)S(1)}, bf16[256,2048]{1,0:T(8,128)(2,1)S(1)}, f32[256,1024]{1,0:T(8,128)S(1)}, f32[256,1024]{1,0:T(8,128)S(1)}, f32[256,1024]{1,0:T(8,128)S(1)}) custom-call(f32[256,1024]{1,0:T(8,128)S(1)} %get-tuple-element.127.refs_0_, f32[256,1024]{1,0:T(8,128)S(1)} %get-tuple-element.128.refs_1_.refs_9_, ...), custom_call_target="tpu_custom_call" | custom-call | flops 268435456 | tf_op jit(solution)/shard_map/pallas_call | solution.py:46
  64.9 3.0 %shard_map.36 = (f32[256,1024]{1,0:T(8,128)S(1)}, f32[256,1024]{1,0:T(8,128)S(1)}, f32[256,1024]{1,0:T(8,128)S(1)}, f32[256,1024]{1,0:T(8,128)S(1)}, f32[40,128]...) custom-call(bf16[256,256]{1,0:T(8,128)(2,1)S(1)} %get-tuple-element.93.refs_0_, ...), custom_call_target="tpu_custom_call" | custom-call | flops 268435456 | tf_op jit(solution)/shard_map/pallas_call | solution.py:46
  71.0 2.1 %collective-permute-done.20.refs_5_ = f32[48,128]{1,0:T(8,128)S(1)} collective-permute-done((f32[48,128]{1,0:T(8,128)S(1)}, f32[48,128]{1,0:T(8,128)S(1)}, u32[]{:S(2)}, u32[]{:S(2)}) %collective-permute-start.20) | collective-permute-done | bytes 24608 | tf_op jit(solution)/shard_map/ppermute | solution.py:614
  74.3 2.4 %shard_map.37 = (f32[256,1024]{1,0:T(8,128)S(1)}, f32[256,1024]{1,0:T(8,128)S(1)}, f32[256,1024]{1,0:T(8,128)S(1)}, f32[256,1024]{1,0:T(8,128)S(1)}, f32[256,128...) custom-call(f32[256,1024]{1,0:T(8,128)S(1)} %get-tuple-element.145.r, ...), custom_call_target="tpu_custom_call" | custom-call | flops 134217728 | tf_op jit(solution)/shard_map/pallas_call | solution.py:46
  76.7 4.3 %collective-permute-start.23 = (f32[16,128]{1,0:T(8,128)S(1)}, f32[16,128]{1,0:T(8,128)S(1)}, u32[]{:S(2)}, u32[]{:S(2)}) collective-permute-start(f32[16,128]{1,0:T(8,128)S(1)} %get-tuple-element.170), channel_id=1, source_target_pairs={{0,24},{1,25},{2,26},{3,27},{4,28},{5,29},{6,30},{7,31},{8,16},{9,... | collective-permute-start | bytes 24584 | tf_op jit(solution)/shard_map/ppermute | solution.py:614
  82.4 1.7 %collective-permute-start.24 = (f32[16,128]{1,0:T(8,128)S(1)}, f32[16,128]{1,0:T(8,128)S(1)}, u32[]{:S(2)}, u32[]{:S(2)}) collective-permute-start(f32[16,128]{1,0:T(8,128)S(1)} %add.59), channel_id=1, source_target_pairs={{0,20},{1,21},{2,22},{3,23},{4,16},{5,17},{6,18},{7,19},{8,28},{9,... | collective-permute-start | bytes 24584 | tf_op jit(solution)/shard_map/ppermute | solution.py:614
  85.5 1.6 %collective-permute-start.25 = (f32[16,128]{1,0:T(8,128)S(1)}, f32[16,128]{1,0:T(8,128)S(1)}, u32[]{:S(2)}, u32[]{:S(2)}) collective-permute-start(f32[16,128]{1,0:T(8,128)S(1)} %add.60), channel_id=1, source_target_pairs={{0,18},{1,19},{2,16},{3,17},{4,22},{5,23},{6,20},{7,21},{8,26},{9,... | collective-permute-start | bytes 24584 | tf_op jit(solution)/shard_map/ppermute | solution.py:614
  88.5 2.5 %collective-permute-start.26 = (f32[16,128]{1,0:T(8,128)S(1)}, f32[16,128]{1,0:T(8,128)S(1)}, u32[]{:S(2)}, u32[]{:S(2)}) collective-permute-start(f32[16,128]{1,0:T(8,128)S(1)} %add.61), channel_id=1, source_target_pairs={{0,17},{1,16},{2,19},{3,18},{4,21},{5,20},{6,23},{7,22},{8,25},{9,... | collective-permute-start | bytes 24584 | tf_op jit(solution)/shard_map/ppermute | solution.py:614
  91.0 1.5 %shard_map.38 = (bf16[256,2048]{1,0:T(8,128)(2,1)S(1)}, bf16[256,2048]{1,0:T(8,128)(2,1)S(1)}) custom-call(f32[256,1024]{1,0:T(8,128)S(1)} %get-tuple-element.153.refs_0_, f32[256,1024]{1,0:T(8,128)S(1)} %get-tuple-element.154.refs_1_, f32[256,1024]{1,0:T(8,128)S(1)} %get-tuple-element.155.refs_2_, f32[256,1024]{1,0:T(8,128)S(1)} %get-tuple-element.156.refs_3_, ...), custom_call_target="tpu_custom_call" | custom-call | flops 268435456 | tf_op jit(solution)/shard_map/pallas_call | solution.py:46
  (68 shorter events, 29.8 us)
Async XLA Ops:
  0.8 4.9 %collective-permute-start.3 = (bf16[32,256]{1,0:T(8,128)(2,1)S(1)}, bf16[32,256]{1,0:T(8,128)(2,1)S(1)}, u32[]{:S(2)}, u32[]{:S(2)}) collective-permute-start(bf16[32,256]{1,0:T(8,128)(2,1)S(1)} %constant_dynamic-slice_fusion.refs_8_), channel_id=1, source_target_pairs={{0,24},{1,25},{2,26},{3,27},{4,28},{5,29},{6,30},{7,31},{8,16},{9,... | collective-permute-start | bytes 49160 | tf_op jit(solution)/shard_map/ppermute | solution.py:614
  5.7 3.5 %collective-permute-start.4 = (bf16[64,256]{1,0:T(8,128)(2,1)S(1)}, bf16[64,256]{1,0:T(8,128)(2,1)S(1)}, u32[]{:S(2)}, u32[]{:S(2)}) collective-permute-start(bf16[64,256]{1,0:T(8,128)(2,1)S(1)} %pad_maximum_fusion.2), channel_id=1, source_target_pairs={{0,20},{1,21},{2,22},{3,23},{4,16},{5,17},{6,18},{7,19},{8,28},{9,... | collective-permute-start | bytes 98312 | tf_op jit(solution)/shard_map/ppermute | solution.py:614
  9.2 5.5 %collective-permute-start.5 = (bf16[128,256]{1,0:T(8,128)(2,1)S(1)}, bf16[128,256]{1,0:T(8,128)(2,1)S(1)}, u32[]{:S(2)}, u32[]{:S(2)}) collective-permute-start(bf16[128,256]{1,0:T(8,128)(2,1)S(1)} %pad_maximum_fusion.1), channel_id=1, source_target_pairs={{0,18},{1,19},{2,16},{3,17},{4,22},{5,23},{6,20},{7,21},{8,26},{9,... | collective-permute-start | bytes 196616 | tf_op jit(solution)/shard_map/ppermute | solution.py:614
  14.2 12.5 %collective-permute-start = (bf16[1024,128]{1,0:T(8,128)(2,1)S(1)}, bf16[1024,128]{1,0:T(8,128)(2,1)S(1)}, u32[]{:S(2)}, u32[]{:S(2)}) collective-permute-start(bf16[1024,128]{1,0:T(8,128)(2,1)S(1)} %get-tuple-element.89), channel_id=1, source_target_pairs={{0,16},{1,17},{2,18},{3,19},{4,20},{5,21},{6,22},{7,23},{8,24},{9,... | collective-permute-start | bytes 786440 | tf_op jit(solution)/shard_map/ppermute | solution.py:614
  14.7 5.6 %collective-permute-start.6 = (bf16[256,256]{1,0:T(8,128)(2,1)S(1)}, bf16[256,256]{1,0:T(8,128)(2,1)S(1)}, u32[]{:S(2)}, u32[]{:S(2)}) collective-permute-start(bf16[256,256]{1,0:T(8,128)(2,1)S(1)} %pad_maximum_fusion.mine.refs_4_), channel_id=1, source_target_pairs={{0,17},{1,16},{2,19},{3,18},{4,21},{5,20},{6,23},{7,22},{8,25},{9,... | collective-permute-start | bytes 393224 | tf_op jit(solution)/shard_map/ppermute | solution.py:614
  16.0 8.5 %collective-permute-start.7 = (bf16[256,256]{1,0:T(8,128)(2,1)S(1)}, bf16[256,256]{1,0:T(8,128)(2,1)S(1)}, u32[]{:S(2)}, u32[]{:S(2)}) collective-permute-start(bf16[256,256]{1,0:T(8,128)(2,1)S(1)} %pad_maximum_fusion.mine.refs_4_), channel_id=1, source_target_pairs={{0,16},{1,17},{2,18},{3,19},{4,20},{5,21},{6,22},{7,23},{8,24},{9,... | collective-permute-start | bytes 393224 | tf_op jit(solution)/shard_map/ppermute | solution.py:614
  20.4 6.4 %collective-permute-start.8 = (bf16[256,256]{1,0:T(8,128)(2,1)S(1)}, bf16[256,256]{1,0:T(8,128)(2,1)S(1)}, u32[]{:S(2)}, u32[]{:S(2)}) collective-permute-start(bf16[256,256]{1,0:T(8,128)(2,1)S(1)} %collective-permute-done.6.refs_5_), channel_id=1, source_target_pairs={{0,16},{1,17},{2,18},{3,19},{4,20},{5,21},{6,22},{7,23},{8,24},{9,... | collective-permute-start | bytes 393224 | tf_op jit(solution)/shard_map/ppermute | solution.py:614
  20.5 4.6 %collective-permute-start.2 = (bf16[16,1024]{1,0:T(8,128)(2,1)S(1)}, bf16[16,1024]{1,0:T(8,128)(2,1)S(1)}, u32[]{:S(2)}, u32[]{:S(2)}) collective-permute-start(bf16[16,1024]{1,0:T(8,128)(2,1)S(1)} %get-tuple-element.90), channel_id=1, source_target_pairs={{1,2},{2,1},{3,4},{4,3},{5,6},{6,5},{7,8},{8,7},{9,10},{10,9},{11,... | collective-permute-start | bytes 98312 | tf_op jit(solution)/shard_map/ppermute | solution.py:652
  21.1 5.6 %collective-permute-start.1 = (bf16[16,1024]{1,0:T(8,128)(2,1)S(1)}, bf16[16,1024]{1,0:T(8,128)(2,1)S(1)}, u32[]{:S(2)}, u32[]{:S(2)}) collective-permute-start(bf16[16,1024]{1,0:T(8,128)(2,1)S(1)} %get-tuple-element.90), channel_id=1, source_target_pairs={{0,1},{1,0},{2,3},{3,2},{4,5},{5,4},{6,7},{7,6},{8,9},{9,8},{10,11... | collective-permute-start | bytes 98312 | tf_op jit(solution)/shard_map/ppermute | solution.py:644
  34.2 4.3 %collective-permute-start.10 = (f32[16,128]{1,0:T(8,128)S(1)}, f32[16,128]{1,0:T(8,128)S(1)}, u32[]{:S(2)}, u32[]{:S(2)}) collective-permute-start(f32[16,128]{1,0:T(8,128)S(1)} %get-tuple-element.124), channel_id=1, source_target_pairs={{0,24},{1,25},{2,26},{3,27},{4,28},{5,29},{6,30},{7,31},{8,16},{9,... | collective-permute-start | bytes 24584 | tf_op jit(solution)/shard_map/ppermute | solution.py:614
  38.6 4.3 %collective-permute-start.11 = (f32[16,128]{1,0:T(8,128)S(1)}, f32[16,128]{1,0:T(8,128)S(1)}, u32[]{:S(2)}, u32[]{:S(2)}) collective-permute-start(f32[16,128]{1,0:T(8,128)S(1)} %add.49), channel_id=1, source_target_pairs={{0,20},{1,21},{2,22},{3,23},{4,16},{5,17},{6,18},{7,19},{8,28},{9,... | collective-permute-start | bytes 24584 | tf_op jit(solution)/shard_map/ppermute | solution.py:614
  42.9 4.3 %collective-permute-start.12 = (f32[16,128]{1,0:T(8,128)S(1)}, f32[16,128]{1,0:T(8,128)S(1)}, u32[]{:S(2)}, u32[]{:S(2)}) collective-permute-start(f32[16,128]{1,0:T(8,128)S(1)} %add.50), channel_id=1, source_target_pairs={{0,18},{1,19},{2,16},{3,17},{4,22},{5,23},{6,20},{7,21},{8,26},{9,... | collective-permute-start | bytes 24584 | tf_op jit(solution)/shard_map/ppermute | solution.py:614
  46.7 5.6 %collective-permute-start.9 = (f32[512,128]{1,0:T(8,128)S(1)}, f32[512,128]{1,0:T(8,128)S(1)}, u32[]{:S(2)}, u32[]{:S(2)}) collective-permute-start(f32[512,128]{1,0:T(8,128)S(1)} %get-tuple-element.123), channel_id=1, source_target_pairs={{0,16},{1,17},{2,18},{3,19},{4,20},{5,21},{6,22},{7,23},{8,24},{9,... | collective-permute-start | bytes 786440 | tf_op jit(solution)/shard_map/ppermute | solution.py:614
  47.2 3.9 %collective-permute-start.13 = (f32[48,128]{1,0:T(8,128)S(1)}, f32[48,128]{1,0:T(8,128)S(1)}, u32[]{:S(2)}, u32[]{:S(2)}) collective-permute-start(f32[48,128]{1,0:T(8,128)S(1)} %pad_maximum_fusion.3), channel_id=1, source_target_pairs={{0,1},{1,0},{2,3},{3,2},{4,5},{5,4},{6,7},{7,6},{8,9},{9,8},{10,11... | collective-permute-start | bytes 73736 | tf_op jit(solution)/shard_map/ppermute | solution.py:614
  48.7 3.6 %collective-permute-start.14 = (f32[32,128]{1,0:T(8,128)S(1)}, f32[32,128]{1,0:T(8,128)S(1)}, u32[]{:S(2)}, u32[]{:S(2)}) collective-permute-start(f32[32,128]{1,0:T(8,128)S(1)} %get-tuple-element.126), channel_id=1, source_target_pairs={{1,2},{2,1},{3,4},{4,3},{5,6},{6,5},{7,8},{8,7},{9,10},{10,9},{11,... | collective-permute-start | bytes 49160 | tf_op jit(solution)/shard_map/ppermute | solution.py:652
  54.7 6.5 %collective-permute-start.17 = (f32[16,128]{1,0:T(8,128)S(1)}, f32[16,128]{1,0:T(8,128)S(1)}, u32[]{:S(2)}, u32[]{:S(2)}) collective-permute-start(f32[16,128]{1,0:T(8,128)S(1)} %get-tuple-element.150), channel_id=1, source_target_pairs={{0,24},{1,25},{2,26},{3,27},{4,28},{5,29},{6,30},{7,31},{8,16},{9,... | collective-permute-start | bytes 24584 | tf_op jit(solution)/shard_map/ppermute | solution.py:614
  61.2 3.4 %collective-permute-start.18 = (f32[16,128]{1,0:T(8,128)S(1)}, f32[16,128]{1,0:T(8,128)S(1)}, u32[]{:S(2)}, u32[]{:S(2)}) collective-permute-start(f32[16,128]{1,0:T(8,128)S(1)} %add.54), channel_id=1, source_target_pairs={{0,20},{1,21},{2,22},{3,23},{4,16},{5,17},{6,18},{7,19},{8,28},{9,... | collective-permute-start | bytes 24584 | tf_op jit(solution)/shard_map/ppermute | solution.py:614
  64.7 4.5 %collective-permute-start.19 = (f32[16,128]{1,0:T(8,128)S(1)}, f32[16,128]{1,0:T(8,128)S(1)}, u32[]{:S(2)}, u32[]{:S(2)}) collective-permute-start(f32[16,128]{1,0:T(8,128)S(1)} %add.55), channel_id=1, source_target_pairs={{0,18},{1,19},{2,16},{3,17},{4,22},{5,23},{6,20},{7,21},{8,26},{9,... | collective-permute-start | bytes 24584 | tf_op jit(solution)/shard_map/ppermute | solution.py:614
  67.8 6.4 %collective-permute-start.16 = (f32[512,128]{1,0:T(8,128)S(1)}, f32[512,128]{1,0:T(8,128)S(1)}, u32[]{:S(2)}, u32[]{:S(2)}) collective-permute-start(f32[512,128]{1,0:T(8,128)S(1)} %get-tuple-element.149), channel_id=1, source_target_pairs={{0,16},{1,17},{2,18},{3,19},{4,20},{5,21},{6,22},{7,23},{8,24},{9,... | collective-permute-start | bytes 786440 | tf_op jit(solution)/shard_map/ppermute | solution.py:614
  69.2 3.9 %collective-permute-start.20 = (f32[48,128]{1,0:T(8,128)S(1)}, f32[48,128]{1,0:T(8,128)S(1)}, u32[]{:S(2)}, u32[]{:S(2)}) collective-permute-start(f32[48,128]{1,0:T(8,128)S(1)} %pad_maximum_fusion.4), channel_id=1, source_target_pairs={{0,1},{1,0},{2,3},{3,2},{4,5},{5,4},{6,7},{7,6},{8,9},{9,8},{10,11... | collective-permute-start | bytes 73736 | tf_op jit(solution)/shard_map/ppermute | solution.py:614
  70.4 3.9 %collective-permute-start.21 = (f32[32,128]{1,0:T(8,128)S(1)}, f32[32,128]{1,0:T(8,128)S(1)}, u32[]{:S(2)}, u32[]{:S(2)}) collective-permute-start(f32[32,128]{1,0:T(8,128)S(1)} %get-tuple-element.152), channel_id=1, source_target_pairs={{1,2},{2,1},{3,4},{4,3},{5,6},{6,5},{7,8},{8,7},{9,10},{10,9},{11,... | collective-permute-start | bytes 49160 | tf_op jit(solution)/shard_map/ppermute | solution.py:652
  76.7 5.7 %collective-permute-start.23 = (f32[16,128]{1,0:T(8,128)S(1)}, f32[16,128]{1,0:T(8,128)S(1)}, u32[]{:S(2)}, u32[]{:S(2)}) collective-permute-start(f32[16,128]{1,0:T(8,128)S(1)} %get-tuple-element.170), channel_id=1, source_target_pairs={{0,24},{1,25},{2,26},{3,27},{4,28},{5,29},{6,30},{7,31},{8,16},{9,... | collective-permute-start | bytes 24584 | tf_op jit(solution)/shard_map/ppermute | solution.py:614
  82.4 3.1 %collective-permute-start.24 = (f32[16,128]{1,0:T(8,128)S(1)}, f32[16,128]{1,0:T(8,128)S(1)}, u32[]{:S(2)}, u32[]{:S(2)}) collective-permute-start(f32[16,128]{1,0:T(8,128)S(1)} %add.59), channel_id=1, source_target_pairs={{0,20},{1,21},{2,22},{3,23},{4,16},{5,17},{6,18},{7,19},{8,28},{9,... | collective-permute-start | bytes 24584 | tf_op jit(solution)/shard_map/ppermute | solution.py:614
  88.5 4.0 %collective-permute-start.26 = (f32[16,128]{1,0:T(8,128)S(1)}, f32[16,128]{1,0:T(8,128)S(1)}, u32[]{:S(2)}, u32[]{:S(2)}) collective-permute-start(f32[16,128]{1,0:T(8,128)S(1)} %add.61), channel_id=1, source_target_pairs={{0,17},{1,16},{2,19},{3,18},{4,21},{5,20},{6,23},{7,22},{8,25},{9,... | collective-permute-start | bytes 24584 | tf_op jit(solution)/shard_map/ppermute | solution.py:614
  (5 other events, 8.1 us)

commit v3 on v2

--- a/solution.py
+++ b/solution.py
@@ -297,13 +297,11 @@
     lane = lanes_of(a[0].shape)
     cols = a[0].shape[1]
     count = len(a) + len(b)
-    first = jnp.zeros_like(a[0])
-    final = jnp.zeros_like(a[0])
+    shown = jnp.zeros_like(a[0])
     for i, value in enumerate(a + b):
-        turned = roll(value, i)
-        first = jnp.where(lane == i, turned, first)
-        final = jnp.where(lane == (i - 1) % cols, turned, final)
-    panel[here, :] = jnp.where(lane < count, first, roll(final, count + 1))
+        shown = jnp.where(lane == i, roll(value, i), shown)
+        shown = jnp.where(lane == count + i, roll(value, count + i + 1 - cols), shown)
+    panel[here, :] = shown
 
 
 def pack_edges(panel, rows, to_pair, to_next):
@@ -544,14 +542,8 @@
     lax.fori_loop(0, count, body, 0, unroll=UNROLL)
 
 
-def solve_kernel(rows, cols, last, *refs):
-    inv_high, inv_low, rhs_high, rhs_low = refs[:4]
-    if last:
-        fit, other = refs[4:]
-    else:
-        side, other_side, multiplier, projected, scalars = refs[4:9]
-        fit, other, fit_gram, other_gram, quad, row_edge, to_pair, to_next, panel = refs[9:]
-    members, pixels = fit.shape
+def solve_kernel(inv_high, inv_low, rhs_high, rhs_low, fit, other):
+    pixels = fit.shape[1]
 
     def store(start, size, value):
         if start < pixels:
@@ -560,8 +552,12 @@
             other[:, start - pixels : start - pixels + size] = value
 
     apply_inverse(inv_high, inv_low, rhs_high, rhs_low, store)
-    if last:
-        return
+
+
+def products_kernel(rows, cols, *refs):
+    fit, other, side, other_side, multiplier, projected, scalars = refs[:7]
+    fit_gram, other_gram, quad, row_edge, to_pair, to_next, panel = refs[7:]
+    members = fit.shape[0]
     shape = (GROUP, cols)
     weight = wide(scalars[0:1, 0:1], shape)
     below = edge_flags()[1]
@@ -773,23 +769,17 @@
             flops=2 * work,
         )
         packed = ((2 * rows * members // cols, cols), F32)
+        fit, other = call(solve_kernel, [field] * 2, [inv_high, inv_low, rhs_high, rhs_low], flops=2 * work)
         if last:
-            outs, more = [], []
-        else:
-            multiplier = sides[2]
-            outs = [field] * 2 + [((5 * GROUP, cols), F32), ((2 * members, cols), F32), packed, packed]
-            more = [*sides, projected, scalars]
-        results_of = call(
-            functools.partial(solve_kernel, rows, cols, last),
-            [field] * 2 + outs,
-            [inv_high, inv_low, rhs_high, rhs_low, *more],
-            [] if last else [pltpu.VMEM(*strip)],
+            break
+        multiplier = sides[2]
+        fit_gram, other_gram, quad, *edge = call(
+            functools.partial(products_kernel, rows, cols),
+            [field] * 2 + [((5 * GROUP, cols), F32), ((2 * members, cols), F32), packed, packed],
+            [fit, other, *sides, projected, scalars],
+            [pltpu.VMEM(*strip)],
             flops=2 * work,
         )
-        fit, other = results_of[:2]
-        if last:
-            break
-        fit_gram, other_gram, quad, *edge = results_of[2:]
         sums, *near = sums_and_halos(residuals, edge)
         norm = results[12]
     (abundance,) = call(

time: 96.2 us -> 93.6 us (0.973)
  starting transfers between devices: 44.3 us -> 42.6 us
  Pallas kernels: 29 us -> 27.8 us
    ppermute x24, starting transfers between devices: 38.9 us -> 37.2 us  [flat_swap(): return lax.ppermute(value, ('row', 'col'), pairs)]
    pallas_call x13 -> x15, Pallas kernels: 29 us -> 27.8 us  [call(): pl.pallas_call(body, out_shape=[jax.ShapeDtypeStruct(*out) for out in out...]
  transfers between devices with their start and end apart: 28 -> 28, of which waited for: 13 -> 16; matrix products, arithmetic and copies ran while one was open for 0% -> 0% of each run, Pallas kernels for 16% -> 15%
where the time goes in v3:
time: 93.6 us; the launch traced here: 93.4 us
  starting transfers between devices  42.6 us (46%)
  Pallas kernels  27.8 us (30%)
  waiting for transfers between devices  21.9 us (23%)
    ppermute x24, starting transfers between devices, flat_swap(): return lax.ppermute(value, ('row', 'col'), pairs)  37.2 us
    pallas_call x15, Pallas kernels, call(): pl.pallas_call(body, out_shape=[jax.ShapeDtypeStruct(*out) for out in out...  27.8 us
    ppermute x24, waiting for transfers between devices, flat_swap(): return lax.ppermute(value, ('row', 'col'), pairs)  20.2 us
    ppermute x1, starting transfers between devices, pair_swap(): lax.ppermute(value, 'col', [(c, c ^ 1) for c in range(count) if c ^ 1 < c...  3.3 us
    ppermute x3, starting transfers between devices, next_swap(): return lax.ppermute(value, 'col', pairs)  2.13 us
  transfers between devices with their start and end apart: 28, of which 16 were waited for; matrix products, arithmetic and copies ran while one was open for 0% of the time, Pallas kernels for 15%

profile of v3, /device:TPU:0, one launch (start us, length us, event | category | flops | bytes accessed | tf_op | source)
XLA Modules:
  0.0 93.4 jit_solution(14700234567474473365)
XLA Ops:
  0.8 3.5 %collective-permute-start.3 = (bf16[32,256]{1,0:T(8,128)(2,1)S(1)}, bf16[32,256]{1,0:T(8,128)(2,1)S(1)}, u32[]{:S(2)}, u32[]{:S(2)}) collective-permute-start(bf16[32,256]{1,0:T(8,128)(2,1)S(1)} %constant_dynamic-slice_fusion.refs_8_), channel_id=1, source_target_pairs={{0,24},{1,25},{2,26},{3,27},{4,28},{5,29},{6,30},{7,31},{8,16},{9,... | collective-permute-start | bytes 49160 | tf_op jit(solution)/shard_map/ppermute | solution.py:610
  5.7 1.9 %collective-permute-start.4 = (bf16[64,256]{1,0:T(8,128)(2,1)S(1)}, bf16[64,256]{1,0:T(8,128)(2,1)S(1)}, u32[]{:S(2)}, u32[]{:S(2)}) collective-permute-start(bf16[64,256]{1,0:T(8,128)(2,1)S(1)} %pad_maximum_fusion.2), channel_id=1, source_target_pairs={{0,20},{1,21},{2,22},{3,23},{4,16},{5,17},{6,18},{7,19},{8,28},{9,... | collective-permute-start | bytes 98312 | tf_op jit(solution)/shard_map/ppermute | solution.py:610
  7.6 1.6 %collective-permute-done.4 = bf16[64,256]{1,0:T(8,128)(2,1)S(1)} collective-permute-done((bf16[64,256]{1,0:T(8,128)(2,1)S(1)}, bf16[64,256]{1,0:T(8,128)(2,1)S(1)}, u32[]{:S(2)}, u32[]{:S(2)}) %collective-permute-start.4) | collective-permute-done | bytes 32800 | tf_op jit(solution)/shard_map/ppermute | solution.py:610
  9.2 1.7 %collective-permute-start.5 = (bf16[128,256]{1,0:T(8,128)(2,1)S(1)}, bf16[128,256]{1,0:T(8,128)(2,1)S(1)}, u32[]{:S(2)}, u32[]{:S(2)}) collective-permute-start(bf16[128,256]{1,0:T(8,128)(2,1)S(1)} %pad_maximum_fusion.1), channel_id=1, source_target_pairs={{0,18},{1,19},{2,16},{3,17},{4,22},{5,23},{6,20},{7,21},{8,26},{9,... | collective-permute-start | bytes 196616 | tf_op jit(solution)/shard_map/ppermute | solution.py:610
  10.9 3.3 %shard_map.28 = (bf16[1024,1024]{1,0:T(8,128)(2,1)S(1)}, bf16[16,1024]{1,0:T(8,128)(2,1)S(1)}, bf16[1024,128]{1,0:T(8,128)(2,1)S(1)}, f32[8,128]{1,0:T(8,128)S(1)}) custom-call(bf16[8192,128]{1,0:T(8,128)(2,1)} %bitcast.2), custom_call_target="tpu_custom_call" | custom-call | flops 16777216 | tf_op jit(solution)/shard_map/pallas_call | solution.py:46
  16.4 3.9 %collective-permute-done.6.refs_5_ = bf16[256,256]{1,0:T(8,128)(2,1)S(1)} collective-permute-done((bf16[256,256]{1,0:T(8,128)(2,1)S(1)}, bf16[256,256]{1,0:T(8,128)(2,1)S(1)}, u32[]{:S(2)}, u32[]{:S(2)}) %collective-permute-start.6) | collective-permute-done | bytes 131104 | tf_op jit(solution)/shard_map/ppermute | solution.py:610
  21.1 3.3 %collective-permute-start.1 = (bf16[16,1024]{1,0:T(8,128)(2,1)S(1)}, bf16[16,1024]{1,0:T(8,128)(2,1)S(1)}, u32[]{:S(2)}, u32[]{:S(2)}) collective-permute-start(bf16[16,1024]{1,0:T(8,128)(2,1)S(1)} %get-tuple-element.90), channel_id=1, source_target_pairs={{0,1},{1,0},{2,3},{3,2},{4,5},{5,4},{6,7},{7,6},{8,9},{9,8},{10,11... | collective-permute-start | bytes 98312 | tf_op jit(solution)/shard_map/ppermute | solution.py:640
  25.0 1.7 %collective-permute-done.1.refs_2_ = bf16[16,1024]{1,0:T(8,128)(2,1)S(1)} collective-permute-done((bf16[16,1024]{1,0:T(8,128)(2,1)S(1)}, bf16[16,1024]{1,0:T(8,128)(2,1)S(1)}, u32[]{:S(2)}, u32[]{:S(2)}) %collective-permute-start.1) | collective-permute-done | bytes 32800 | tf_op jit(solution)/shard_map/ppermute | solution.py:640
  26.7 6.2 %shard_map.30 = (f32[256,1024]{1,0:T(8,128)S(1)}, bf16[256,256]{1,0:T(8,128)(2,1)S(1)}, bf16[256,256]{1,0:T(8,128)(2,1)S(1)}, f32[256,1024]{1,0:T(8,128)S(1)}, f...) custom-call(bf16[1024,1024]{1,0:T(8,128)(2,1)S(1)} %get-tuple-elemen, ...), custom_call_target="tpu_custom_call" | custom-call | flops 1073741824 | tf_op jit(solution)/shard_map/pallas_call | solution.py:46
  34.2 2.9 %collective-permute-start.10 = (f32[16,128]{1,0:T(8,128)S(1)}, f32[16,128]{1,0:T(8,128)S(1)}, u32[]{:S(2)}, u32[]{:S(2)}) collective-permute-start(f32[16,128]{1,0:T(8,128)S(1)} %get-tuple-element.124), channel_id=1, source_target_pairs={{0,24},{1,25},{2,26},{3,27},{4,28},{5,29},{6,30},{7,31},{8,16},{9,... | collective-permute-start | bytes 24584 | tf_op jit(solution)/shard_map/ppermute | solution.py:610
  37.2 1.5 %shard_map.32 = (bf16[256,2048]{1,0:T(8,128)(2,1)S(1)}, bf16[256,2048]{1,0:T(8,128)(2,1)S(1)}, f32[256,1024]{1,0:T(8,128)S(1)}, f32[256,1024]{1,0:T(8,128)S(1)}, f32[256,1024]{1,0:T(8,128)S(1)}) custom-call(f32[256,1024]{1,0:T(8,128)S(1)} %get-tuple-element.101.refs_0_, f32[256,1024]{1,0:T(8,128)S(1)} %get-tuple-element.102.refs_1_.refs_9_, ...), custom_call_target="tpu_custom_call" | custom-call | flops 268435456 | tf_op jit(solution)/shard_map/pallas_call | solution.py:46
  38.7 3.0 %collective-permute-start.11 = (f32[16,128]{1,0:T(8,128)S(1)}, f32[16,128]{1,0:T(8,128)S(1)}, u32[]{:S(2)}, u32[]{:S(2)}) collective-permute-start(f32[16,128]{1,0:T(8,128)S(1)} %add.49), channel_id=1, source_target_pairs={{0,20},{1,21},{2,22},{3,23},{4,16},{5,17},{6,18},{7,19},{8,28},{9,... | collective-permute-start | bytes 24584 | tf_op jit(solution)/shard_map/ppermute | solution.py:610
  48.0 1.9 %collective-permute-done.13.refs_5_ = f32[48,128]{1,0:T(8,128)S(1)} collective-permute-done((f32[48,128]{1,0:T(8,128)S(1)}, f32[48,128]{1,0:T(8,128)S(1)}, u32[]{:S(2)}, u32[]{:S(2)}) %collective-permute-start.13) | collective-permute-done | bytes 24608 | tf_op jit(solution)/shard_map/ppermute | solution.py:610
  51.1 2.4 %shard_map.35 = (f32[256,1024]{1,0:T(8,128)S(1)}, f32[256,1024]{1,0:T(8,128)S(1)}, f32[256,1024]{1,0:T(8,128)S(1)}, f32[256,1024]{1,0:T(8,128)S(1)}, f32[256,128...) custom-call(f32[256,1024]{1,0:T(8,128)S(1)} %get-tuple-element.116.r, ...), custom_call_target="tpu_custom_call" | custom-call | flops 134217728 | tf_op jit(solution)/shard_map/pallas_call | solution.py:46
  53.6 4.7 %collective-permute-start.17 = (f32[16,128]{1,0:T(8,128)S(1)}, f32[16,128]{1,0:T(8,128)S(1)}, u32[]{:S(2)}, u32[]{:S(2)}) collective-permute-start(f32[16,128]{1,0:T(8,128)S(1)} %get-tuple-element.150), channel_id=1, source_target_pairs={{0,24},{1,25},{2,26},{3,27},{4,28},{5,29},{6,30},{7,31},{8,16},{9,... | collective-permute-start | bytes 24584 | tf_op jit(solution)/shard_map/ppermute | solution.py:610
  58.2 1.6 %shard_map.36 = (bf16[256,2048]{1,0:T(8,128)(2,1)S(1)}, bf16[256,2048]{1,0:T(8,128)(2,1)S(1)}, f32[256,1024]{1,0:T(8,128)S(1)}, f32[256,1024]{1,0:T(8,128)S(1)}, f32[256,1024]{1,0:T(8,128)S(1)}) custom-call(f32[256,1024]{1,0:T(8,128)S(1)} %get-tuple-element.127.refs_0_, f32[256,1024]{1,0:T(8,128)S(1)} %get-tuple-element.128.refs_1_.refs_9_, ...), custom_call_target="tpu_custom_call" | custom-call | flops 268435456 | tf_op jit(solution)/shard_map/pallas_call | solution.py:46
  59.8 2.6 %collective-permute-start.18 = (f32[16,128]{1,0:T(8,128)S(1)}, f32[16,128]{1,0:T(8,128)S(1)}, u32[]{:S(2)}, u32[]{:S(2)}) collective-permute-start(f32[16,128]{1,0:T(8,128)S(1)} %add.54), channel_id=1, source_target_pairs={{0,20},{1,21},{2,22},{3,23},{4,16},{5,17},{6,18},{7,19},{8,28},{9,... | collective-permute-start | bytes 24584 | tf_op jit(solution)/shard_map/ppermute | solution.py:610
  68.6 2.2 %collective-permute-done.20.refs_5_ = f32[48,128]{1,0:T(8,128)S(1)} collective-permute-done((f32[48,128]{1,0:T(8,128)S(1)}, f32[48,128]{1,0:T(8,128)S(1)}, u32[]{:S(2)}, u32[]{:S(2)}) %collective-permute-start.20) | collective-permute-done | bytes 24608 | tf_op jit(solution)/shard_map/ppermute | solution.py:610
  72.1 2.4 %shard_map.39 = (f32[256,1024]{1,0:T(8,128)S(1)}, f32[256,1024]{1,0:T(8,128)S(1)}, f32[256,1024]{1,0:T(8,128)S(1)}, f32[256,1024]{1,0:T(8,128)S(1)}, f32[256,128...) custom-call(f32[256,1024]{1,0:T(8,128)S(1)} %get-tuple-element.142.r, ...), custom_call_target="tpu_custom_call" | custom-call | flops 134217728 | tf_op jit(solution)/shard_map/pallas_call | solution.py:46
  74.5 4.0 %collective-permute-start.23 = (f32[16,128]{1,0:T(8,128)S(1)}, f32[16,128]{1,0:T(8,128)S(1)}, u32[]{:S(2)}, u32[]{:S(2)}) collective-permute-start(f32[16,128]{1,0:T(8,128)S(1)} %get-tuple-element.170), channel_id=1, source_target_pairs={{0,24},{1,25},{2,26},{3,27},{4,28},{5,29},{6,30},{7,31},{8,16},{9,... | collective-permute-start | bytes 24584 | tf_op jit(solution)/shard_map/ppermute | solution.py:610
  79.8 3.0 %collective-permute-start.24 = (f32[16,128]{1,0:T(8,128)S(1)}, f32[16,128]{1,0:T(8,128)S(1)}, u32[]{:S(2)}, u32[]{:S(2)}) collective-permute-start(f32[16,128]{1,0:T(8,128)S(1)} %add.59), channel_id=1, source_target_pairs={{0,20},{1,21},{2,22},{3,23},{4,16},{5,17},{6,18},{7,19},{8,28},{9,... | collective-permute-start | bytes 24584 | tf_op jit(solution)/shard_map/ppermute | solution.py:610
  85.1 2.1 %collective-permute-done.25 = f32[16,128]{1,0:T(8,128)S(1)} collective-permute-done((f32[16,128]{1,0:T(8,128)S(1)}, f32[16,128]{1,0:T(8,128)S(1)}, u32[]{:S(2)}, u32[]{:S(2)}) %collective-permute-start.25) | collective-permute-done | bytes 8224 | tf_op jit(solution)/shard_map/ppermute | solution.py:610
  88.4 1.5 %shard_map.40 = (bf16[256,2048]{1,0:T(8,128)(2,1)S(1)}, bf16[256,2048]{1,0:T(8,128)(2,1)S(1)}) custom-call(f32[256,1024]{1,0:T(8,128)S(1)} %get-tuple-element.153.refs_0_, f32[256,1024]{1,0:T(8,128)S(1)} %get-tuple-element.154.refs_1_, f32[256,1024]{1,0:T(8,128)S(1)} %get-tuple-element.155.refs_2_, f32[256,1024]{1,0:T(8,128)S(1)} %get-tuple-element.156.refs_3_, ...), custom_call_target="tpu_custom_call" | custom-call | flops 268435456 | tf_op jit(solution)/shard_map/pallas_call | solution.py:46
  91.9 1.5 %shard_map.42 = f32[2048,128]{1,0:T(8,128)} custom-call(f32[256,1024]{1,0:T(8,128)S(1)} %get-tuple-element.168.fit, f32[256,1024]{1,0:T(8,128)S(1)} %get-tuple-element.169.other, f32[8,128]{1,0:T(8,128)S(1)} %get-tuple-element.163.refs_10_.scalars, f32[16,128]{1,0:T(8,128)S(1)} %add.63.sums), custom_call_target="tpu_custom_call" | custom-call | flops 16777216 | tf_op jit(solution)/shard_map/pallas_call | solution.py:46
  (70 shorter events, 28.8 us)
Async XLA Ops:
  0.8 4.9 %collective-permute-start.3 = (bf16[32,256]{1,0:T(8,128)(2,1)S(1)}, bf16[32,256]{1,0:T(8,128)(2,1)S(1)}, u32[]{:S(2)}, u32[]{:S(2)}) collective-permute-start(bf16[32,256]{1,0:T(8,128)(2,1)S(1)} %constant_dynamic-slice_fusion.refs_8_), channel_id=1, source_target_pairs={{0,24},{1,25},{2,26},{3,27},{4,28},{5,29},{6,30},{7,31},{8,16},{9,... | collective-permute-start | bytes 49160 | tf_op jit(solution)/shard_map/ppermute | solution.py:610
  5.7 3.5 %collective-permute-start.4 = (bf16[64,256]{1,0:T(8,128)(2,1)S(1)}, bf16[64,256]{1,0:T(8,128)(2,1)S(1)}, u32[]{:S(2)}, u32[]{:S(2)}) collective-permute-start(bf16[64,256]{1,0:T(8,128)(2,1)S(1)} %pad_maximum_fusion.2), channel_id=1, source_target_pairs={{0,20},{1,21},{2,22},{3,23},{4,16},{5,17},{6,18},{7,19},{8,28},{9,... | collective-permute-start | bytes 98312 | tf_op jit(solution)/shard_map/ppermute | solution.py:610
  9.2 5.5 %collective-permute-start.5 = (bf16[128,256]{1,0:T(8,128)(2,1)S(1)}, bf16[128,256]{1,0:T(8,128)(2,1)S(1)}, u32[]{:S(2)}, u32[]{:S(2)}) collective-permute-start(bf16[128,256]{1,0:T(8,128)(2,1)S(1)} %pad_maximum_fusion.1), channel_id=1, source_target_pairs={{0,18},{1,19},{2,16},{3,17},{4,22},{5,23},{6,20},{7,21},{8,26},{9,... | collective-permute-start | bytes 196616 | tf_op jit(solution)/shard_map/ppermute | solution.py:610
  14.2 12.5 %collective-permute-start = (bf16[1024,128]{1,0:T(8,128)(2,1)S(1)}, bf16[1024,128]{1,0:T(8,128)(2,1)S(1)}, u32[]{:S(2)}, u32[]{:S(2)}) collective-permute-start(bf16[1024,128]{1,0:T(8,128)(2,1)S(1)} %get-tuple-element.89), channel_id=1, source_target_pairs={{0,16},{1,17},{2,18},{3,19},{4,20},{5,21},{6,22},{7,23},{8,24},{9,... | collective-permute-start | bytes 786440 | tf_op jit(solution)/shard_map/ppermute | solution.py:610
  14.7 5.6 %collective-permute-start.6 = (bf16[256,256]{1,0:T(8,128)(2,1)S(1)}, bf16[256,256]{1,0:T(8,128)(2,1)S(1)}, u32[]{:S(2)}, u32[]{:S(2)}) collective-permute-start(bf16[256,256]{1,0:T(8,128)(2,1)S(1)} %pad_maximum_fusion.mine.refs_4_), channel_id=1, source_target_pairs={{0,17},{1,16},{2,19},{3,18},{4,21},{5,20},{6,23},{7,22},{8,25},{9,... | collective-permute-start | bytes 393224 | tf_op jit(solution)/shard_map/ppermute | solution.py:610
  16.0 8.5 %collective-permute-start.7 = (bf16[256,256]{1,0:T(8,128)(2,1)S(1)}, bf16[256,256]{1,0:T(8,128)(2,1)S(1)}, u32[]{:S(2)}, u32[]{:S(2)}) collective-permute-start(bf16[256,256]{1,0:T(8,128)(2,1)S(1)} %pad_maximum_fusion.mine.refs_4_), channel_id=1, source_target_pairs={{0,16},{1,17},{2,18},{3,19},{4,20},{5,21},{6,22},{7,23},{8,24},{9,... | collective-permute-start | bytes 393224 | tf_op jit(solution)/shard_map/ppermute | solution.py:610
  20.4 6.4 %collective-permute-start.8 = (bf16[256,256]{1,0:T(8,128)(2,1)S(1)}, bf16[256,256]{1,0:T(8,128)(2,1)S(1)}, u32[]{:S(2)}, u32[]{:S(2)}) collective-permute-start(bf16[256,256]{1,0:T(8,128)(2,1)S(1)} %collective-permute-done.6.refs_5_), channel_id=1, source_target_pairs={{0,16},{1,17},{2,18},{3,19},{4,20},{5,21},{6,22},{7,23},{8,24},{9,... | collective-permute-start | bytes 393224 | tf_op jit(solution)/shard_map/ppermute | solution.py:610
  20.5 4.6 %collective-permute-start.2 = (bf16[16,1024]{1,0:T(8,128)(2,1)S(1)}, bf16[16,1024]{1,0:T(8,128)(2,1)S(1)}, u32[]{:S(2)}, u32[]{:S(2)}) collective-permute-start(bf16[16,1024]{1,0:T(8,128)(2,1)S(1)} %get-tuple-element.90), channel_id=1, source_target_pairs={{1,2},{2,1},{3,4},{4,3},{5,6},{6,5},{7,8},{8,7},{9,10},{10,9},{11,... | collective-permute-start | bytes 98312 | tf_op jit(solution)/shard_map/ppermute | solution.py:648
  21.1 5.6 %collective-permute-start.1 = (bf16[16,1024]{1,0:T(8,128)(2,1)S(1)}, bf16[16,1024]{1,0:T(8,128)(2,1)S(1)}, u32[]{:S(2)}, u32[]{:S(2)}) collective-permute-start(bf16[16,1024]{1,0:T(8,128)(2,1)S(1)} %get-tuple-element.90), channel_id=1, source_target_pairs={{0,1},{1,0},{2,3},{3,2},{4,5},{5,4},{6,7},{7,6},{8,9},{9,8},{10,11... | collective-permute-start | bytes 98312 | tf_op jit(solution)/shard_map/ppermute | solution.py:640
  34.2 4.4 %collective-permute-start.10 = (f32[16,128]{1,0:T(8,128)S(1)}, f32[16,128]{1,0:T(8,128)S(1)}, u32[]{:S(2)}, u32[]{:S(2)}) collective-permute-start(f32[16,128]{1,0:T(8,128)S(1)} %get-tuple-element.124), channel_id=1, source_target_pairs={{0,24},{1,25},{2,26},{3,27},{4,28},{5,29},{6,30},{7,31},{8,16},{9,... | collective-permute-start | bytes 24584 | tf_op jit(solution)/shard_map/ppermute | solution.py:610
  38.7 4.3 %collective-permute-start.11 = (f32[16,128]{1,0:T(8,128)S(1)}, f32[16,128]{1,0:T(8,128)S(1)}, u32[]{:S(2)}, u32[]{:S(2)}) collective-permute-start(f32[16,128]{1,0:T(8,128)S(1)} %add.49), channel_id=1, source_target_pairs={{0,20},{1,21},{2,22},{3,23},{4,16},{5,17},{6,18},{7,19},{8,28},{9,... | collective-permute-start | bytes 24584 | tf_op jit(solution)/shard_map/ppermute | solution.py:610
  43.0 3.1 %collective-permute-start.12 = (f32[16,128]{1,0:T(8,128)S(1)}, f32[16,128]{1,0:T(8,128)S(1)}, u32[]{:S(2)}, u32[]{:S(2)}) collective-permute-start(f32[16,128]{1,0:T(8,128)S(1)} %add.50), channel_id=1, source_target_pairs={{0,18},{1,19},{2,16},{3,17},{4,22},{5,23},{6,20},{7,21},{8,26},{9,... | collective-permute-start | bytes 24584 | tf_op jit(solution)/shard_map/ppermute | solution.py:610
  45.3 5.8 %collective-permute-start.9 = (f32[512,128]{1,0:T(8,128)S(1)}, f32[512,128]{1,0:T(8,128)S(1)}, u32[]{:S(2)}, u32[]{:S(2)}) collective-permute-start(f32[512,128]{1,0:T(8,128)S(1)} %get-tuple-element.123), channel_id=1, source_target_pairs={{0,16},{1,17},{2,18},{3,19},{4,20},{5,21},{6,22},{7,23},{8,24},{9,... | collective-permute-start | bytes 786440 | tf_op jit(solution)/shard_map/ppermute | solution.py:610
  46.1 3.8 %collective-permute-start.13 = (f32[48,128]{1,0:T(8,128)S(1)}, f32[48,128]{1,0:T(8,128)S(1)}, u32[]{:S(2)}, u32[]{:S(2)}) collective-permute-start(f32[48,128]{1,0:T(8,128)S(1)} %pad_maximum_fusion.3), channel_id=1, source_target_pairs={{0,1},{1,0},{2,3},{3,2},{4,5},{5,4},{6,7},{7,6},{8,9},{9,8},{10,11... | collective-permute-start | bytes 73736 | tf_op jit(solution)/shard_map/ppermute | solution.py:610
  47.3 3.8 %collective-permute-start.14 = (f32[32,128]{1,0:T(8,128)S(1)}, f32[32,128]{1,0:T(8,128)S(1)}, u32[]{:S(2)}, u32[]{:S(2)}) collective-permute-start(f32[32,128]{1,0:T(8,128)S(1)} %get-tuple-element.126), channel_id=1, source_target_pairs={{1,2},{2,1},{3,4},{4,3},{5,6},{6,5},{7,8},{8,7},{9,10},{10,9},{11,... | collective-permute-start | bytes 49160 | tf_op jit(solution)/shard_map/ppermute | solution.py:648
  53.6 6.2 %collective-permute-start.17 = (f32[16,128]{1,0:T(8,128)S(1)}, f32[16,128]{1,0:T(8,128)S(1)}, u32[]{:S(2)}, u32[]{:S(2)}) collective-permute-start(f32[16,128]{1,0:T(8,128)S(1)} %get-tuple-element.150), channel_id=1, source_target_pairs={{0,24},{1,25},{2,26},{3,27},{4,28},{5,29},{6,30},{7,31},{8,16},{9,... | collective-permute-start | bytes 24584 | tf_op jit(solution)/shard_map/ppermute | solution.py:610
  59.8 4.0 %collective-permute-start.18 = (f32[16,128]{1,0:T(8,128)S(1)}, f32[16,128]{1,0:T(8,128)S(1)}, u32[]{:S(2)}, u32[]{:S(2)}) collective-permute-start(f32[16,128]{1,0:T(8,128)S(1)} %add.54), channel_id=1, source_target_pairs={{0,20},{1,21},{2,22},{3,23},{4,16},{5,17},{6,18},{7,19},{8,28},{9,... | collective-permute-start | bytes 24584 | tf_op jit(solution)/shard_map/ppermute | solution.py:610
  63.8 3.1 %collective-permute-start.19 = (f32[16,128]{1,0:T(8,128)S(1)}, f32[16,128]{1,0:T(8,128)S(1)}, u32[]{:S(2)}, u32[]{:S(2)}) collective-permute-start(f32[16,128]{1,0:T(8,128)S(1)} %add.55), channel_id=1, source_target_pairs={{0,18},{1,19},{2,16},{3,17},{4,22},{5,23},{6,20},{7,21},{8,26},{9,... | collective-permute-start | bytes 24584 | tf_op jit(solution)/shard_map/ppermute | solution.py:610
  66.4 5.6 %collective-permute-start.16 = (f32[512,128]{1,0:T(8,128)S(1)}, f32[512,128]{1,0:T(8,128)S(1)}, u32[]{:S(2)}, u32[]{:S(2)}) collective-permute-start(f32[512,128]{1,0:T(8,128)S(1)} %get-tuple-element.149), channel_id=1, source_target_pairs={{0,16},{1,17},{2,18},{3,19},{4,20},{5,21},{6,22},{7,23},{8,24},{9,... | collective-permute-start | bytes 786440 | tf_op jit(solution)/shard_map/ppermute | solution.py:610
  66.9 4.0 %collective-permute-start.20 = (f32[48,128]{1,0:T(8,128)S(1)}, f32[48,128]{1,0:T(8,128)S(1)}, u32[]{:S(2)}, u32[]{:S(2)}) collective-permute-start(f32[48,128]{1,0:T(8,128)S(1)} %pad_maximum_fusion.4), channel_id=1, source_target_pairs={{0,1},{1,0},{2,3},{3,2},{4,5},{5,4},{6,7},{7,6},{8,9},{9,8},{10,11... | collective-permute-start | bytes 73736 | tf_op jit(solution)/shard_map/ppermute | solution.py:610
  67.8 4.2 %collective-permute-start.21 = (f32[32,128]{1,0:T(8,128)S(1)}, f32[32,128]{1,0:T(8,128)S(1)}, u32[]{:S(2)}, u32[]{:S(2)}) collective-permute-start(f32[32,128]{1,0:T(8,128)S(1)} %get-tuple-element.152), channel_id=1, source_target_pairs={{1,2},{2,1},{3,4},{4,3},{5,6},{6,5},{7,8},{8,7},{9,10},{10,9},{11,... | collective-permute-start | bytes 49160 | tf_op jit(solution)/shard_map/ppermute | solution.py:648
  74.5 5.3 %collective-permute-start.23 = (f32[16,128]{1,0:T(8,128)S(1)}, f32[16,128]{1,0:T(8,128)S(1)}, u32[]{:S(2)}, u32[]{:S(2)}) collective-permute-start(f32[16,128]{1,0:T(8,128)S(1)} %get-tuple-element.170), channel_id=1, source_target_pairs={{0,24},{1,25},{2,26},{3,27},{4,28},{5,29},{6,30},{7,31},{8,16},{9,... | collective-permute-start | bytes 24584 | tf_op jit(solution)/shard_map/ppermute | solution.py:610
  79.8 4.3 %collective-permute-start.24 = (f32[16,128]{1,0:T(8,128)S(1)}, f32[16,128]{1,0:T(8,128)S(1)}, u32[]{:S(2)}, u32[]{:S(2)}) collective-permute-start(f32[16,128]{1,0:T(8,128)S(1)} %add.59), channel_id=1, source_target_pairs={{0,20},{1,21},{2,22},{3,23},{4,16},{5,17},{6,18},{7,19},{8,28},{9,... | collective-permute-start | bytes 24584 | tf_op jit(solution)/shard_map/ppermute | solution.py:610
  87.2 3.1 %collective-permute-start.26 = (f32[16,128]{1,0:T(8,128)S(1)}, f32[16,128]{1,0:T(8,128)S(1)}, u32[]{:S(2)}, u32[]{:S(2)}) collective-permute-start(f32[16,128]{1,0:T(8,128)S(1)} %add.61), channel_id=1, source_target_pairs={{0,17},{1,16},{2,19},{3,18},{4,21},{5,20},{6,23},{7,22},{8,25},{9,... | collective-permute-start | bytes 24584 | tf_op jit(solution)/shard_map/ppermute | solution.py:610
  (5 other events, 7.8 us)
